TPU v7x, 512 devices: a whole 4x8x8 slice. The times are simulated.
512 devices in a mesh: wide: 128 (over z, y, core), narrow: 4 (over x).
Axes of the slice: x: 4, y: 8, z: 8, core: 2. Of those that a mesh axis runs over, the one named last changes fastest.
Arguments:
- mesh_latent: bfloat16 [32768, 512], P(('wide', 'narrow')), may hold values from -6 to 6
- mesh_edges: bfloat16 [262144, 512], P(('wide', 'narrow')), may hold values from -6 to 6
- grid_latent: bfloat16 [131072, 512], P(('wide', 'narrow')), may hold values from -6 to 6
- decoder_edges: bfloat16 [393216, 512], P(('wide', 'narrow')), may hold values from -6 to 6
- mesh_senders: int32 [32768, 8], P(('wide', 'narrow')), may hold values from 0 to 4351
- mesh_degree: int32 [32768], P(('wide', 'narrow')), may hold values from 1 to 8
- decoder_senders: int32 [131072, 3], P(('wide', 'narrow')), may hold values from 0 to 319
- mesh_send_rows: int32 [128, 4, 128, 32], P('wide', 'narrow'), may hold values from 0 to 255
- decoder_send_rows: int32 [128, 4, 2, 32], P('wide', 'narrow'), may hold values from 0 to 255
- proc_edge_in: bfloat16 [1536, 512], P('wide'), may hold values from -0.15625 to 0.15625
- proc_edge_out: bfloat16 [512, 512], P('wide'), may hold values from -0.25 to 0.25
- proc_node_in: bfloat16 [1024, 512], P('wide'), may hold values from -0.1875 to 0.1875
- proc_node_out: bfloat16 [512, 512], P('wide'), may hold values from -0.25 to 0.25
- dec_edge_in: bfloat16 [1536, 512], P('wide'), may hold values from -0.15625 to 0.15625
- dec_edge_out: bfloat16 [512, 512], P('wide'), may hold values from -0.25 to 0.25
- grid_node_in: bfloat16 [1024, 512], P('wide'), may hold values from -0.1875 to 0.1875
- grid_node_out: bfloat16 [512, 512], P('wide'), may hold values from -0.25 to 0.25
- output_head: bfloat16 [512, 227], P('wide'), may hold values from -0.25 to 0.25
Outputs:
- mesh_out: bfloat16 [32768, 512], P(('wide', 'narrow'))
- edge_out: bfloat16 [262144, 512], P(('wide', 'narrow'))
- grid_pred: float32 [131072, 227], P(('wide', 'narrow'))
Inputs may be any that keep to these rules, and one draw needn't show every extreme that they name: `mesh_senders`: slots name rows of the device's sender table: below 256 its own patch, above it 32 rows supplied by each patch in turn. A mesh node's live edges are its first mesh_degree slots. `decoder_senders`: slots name rows of the device's decoder sender table: below 256 its own patch, then 32 rows from the previous patch and 32 rows from the next patch. `mesh_send_rows`: entry [p, n, q, k] is a row of patch p. `decoder_send_rows`: entry [p, n, j, k] is a row of patch p.
All inputs are finite; a program needn't handle non-finite values.
Results may differ from a plain program's by a relative error of at most 0.012.
Values may be sent and summed in bfloat16 or wider, within the bound.
No kernel may reach another device: no remote copies, remote signals or barrier semaphores. Data moves between devices by JAX's collectives and lax.ppermute only.
A program may use at most 64 MiB of HBM per device.

v0:
```python
import jax
import jax.numpy as jnp
from jax import lax
from jax.sharding import PartitionSpec as P


def sent_together(arrays, axis, dim, along):
    widths = [a.shape[along] for a in arrays]
    both = jnp.concatenate(arrays, axis=along)
    whole = lax.all_gather(both, axis, axis=dim, tiled=True)
    return tuple(jnp.split(whole, [sum(widths[:k]) for k in range(1, len(widths))], axis=along))


def split_up(shard, dim, count):
    before, after = (shard.shape[:dim], shard.shape[dim + 1 :])
    return jnp.moveaxis(shard.reshape(*before, count, -1, *after), dim, 0)


def cut_rows(length, count):
    unit = 8 if length >= 8 * count else 1
    return [length // unit * k // count * unit for k in range(1, count)]


def in_order(blocks, dim):
    lengths = list(blocks.shape[1:])
    lengths[dim] *= blocks.shape[0]
    return jnp.moveaxis(blocks, 0, dim).reshape(lengths)


def several_exchanges(shard, axis, pieces, split_dim, concat_dim):
    blocks = split_up(shard, split_dim, lax.axis_size(axis))
    split_at = max(range(1, max(2, blocks.ndim - 1)), key=lambda d: blocks.shape[d])
    done = []
    for share in jnp.split(blocks, cut_rows(blocks.shape[split_at], pieces), axis=split_at):
        if share.size:
            done.append(lax.all_to_all(share, axis, split_axis=0, concat_axis=0, tiled=True))
    return in_order(jnp.concatenate(done, axis=split_at), concat_dim)


def from_everyone(shard, axis):
    copies = jnp.broadcast_to(shard, (lax.axis_size(axis), *shard.shape))
    return lax.all_to_all(copies, axis, split_axis=0, concat_axis=0, tiled=True)


def gather_directly(shard, axis, dim):
    blocks = from_everyone(shard, axis)
    return in_order(blocks, dim)


def passed_along(block, axis, distance):
    devices = range(lax.axis_size(axis))
    route = [((i - distance) % len(devices), i) for i in devices]
    return lax.ppermute(block, axis, route)


def swish(values):
    return values * jax.nn.sigmoid(values)


def normalize(values):
    center = values - jnp.mean(values, axis=-1, keepdims=True)
    spread = jnp.mean(center * center, axis=-1, keepdims=True)
    return center * lax.rsqrt(spread + 1e-05)


def second_layer(hidden_pre, w_second):
    active = swish(hidden_pre).astype(jnp.bfloat16)
    return normalize(jnp.dot(active, w_second, preferred_element_type=jnp.float32))


def edge_update(edges, w_edge, w_second, rows, receiver_term, degree):
    width = edges.shape[1]
    pre = jnp.dot(edges, w_edge, preferred_element_type=jnp.float32).reshape(-1, degree, width)
    pre = pre + rows.reshape(-1, degree, width) + receiver_term[:, None, :]
    return (edges + second_layer(pre.reshape(-1, width), w_second)).astype(jnp.bfloat16)


def node_update(latent, summed, w_first, w_second):
    width = latent.shape[1]
    pre = jnp.dot(latent, w_first[:width], preferred_element_type=jnp.float32)
    pre = pre + jnp.dot(summed, w_first[width:], preferred_element_type=jnp.float32)
    return (latent + second_layer(pre, w_second)).astype(jnp.bfloat16)


def body(
    mesh_latent,
    mesh_edges,
    grid_latent,
    decoder_edges,
    mesh_senders,
    mesh_degree,
    decoder_senders,
    mesh_send_rows,
    decoder_send_rows,
    proc_edge_in,
    proc_edge_out,
    proc_node_in,
    proc_node_out,
    dec_edge_in,
    dec_edge_out,
    grid_node_in,
    grid_node_out,
    output_head,
):
    width = mesh_latent.shape[1]
    peers = lax.axis_size("wide")
    gathered = (
        lax.all_gather(proc_edge_in, "wide", axis=0, tiled=True),
        lax.all_gather(proc_edge_out, "wide", axis=0, tiled=True),
        lax.all_gather(proc_node_in, "wide", axis=0, tiled=True),
        lax.all_gather(proc_node_out, "wide", axis=0, tiled=True),
        lax.all_gather(dec_edge_in, "wide", axis=0, tiled=True),
        lax.all_gather(dec_edge_out, "wide", axis=0, tiled=True),
        lax.all_gather(grid_node_in, "wide", axis=0, tiled=True),
        *sent_together((grid_node_out, output_head), "wide", 0, 1),
    )
    (
        pe_first,
        pe_second,
        pn_first,
        pn_second,
        de_first,
        de_second,
        gn_first,
        gn_second,
        head_full,
    ) = gathered
    w_send = pe_first[width : 2 * width]
    patch = lax.all_gather(mesh_latent, "narrow", axis=0, tiled=True)
    outgoing = jnp.take(patch, mesh_send_rows.reshape(-1), axis=0).reshape(peers, -1, width)
    incoming = several_exchanges(outgoing, "wide", 2, 0, 0)
    table = jnp.concatenate([patch, incoming.reshape(-1, width)], axis=0)
    table = jnp.dot(table, w_send, preferred_element_type=jnp.float32).astype(jnp.bfloat16)
    degree = mesh_senders.shape[1]
    rows = jnp.take(table, mesh_senders.reshape(-1), axis=0)
    receiver_term = jnp.dot(mesh_latent, pe_first[2 * width :], preferred_element_type=jnp.float32)
    edge_out = edge_update(mesh_edges, pe_first[:width], pe_second, rows, receiver_term, degree)
    live = (
        lax.broadcasted_iota(jnp.int32, (mesh_degree.shape[0], degree), 1) < mesh_degree[:, None]
    ).astype(jnp.float32)
    summed = jnp.sum(
        edge_out.reshape(-1, degree, width).astype(jnp.float32) * live[:, :, None], axis=1
    ).astype(jnp.bfloat16)
    mesh_out = node_update(mesh_latent, summed, pn_first, pn_second)
    w_dsend = de_first[width : 2 * width]
    dpatch = gather_directly(mesh_out, "narrow", 0)
    doutgoing = jnp.take(dpatch, decoder_send_rows.reshape(-1), axis=0).reshape(2, -1, width)
    from_below = passed_along(doutgoing[0], "wide", 1)
    from_above = passed_along(doutgoing[1], "wide", -1)
    dtable = jnp.concatenate([dpatch, from_below, from_above], axis=0)
    dtable = jnp.dot(dtable, w_dsend, preferred_element_type=jnp.float32).astype(jnp.bfloat16)
    dfanin = decoder_senders.shape[1]
    drows = jnp.take(dtable, decoder_senders.reshape(-1), axis=0)
    grid_term = jnp.dot(grid_latent, de_first[2 * width :], preferred_element_type=jnp.float32)
    dedge = edge_update(decoder_edges, de_first[:width], de_second, drows, grid_term, dfanin)
    gsummed = jnp.sum(dedge.reshape(-1, dfanin, width).astype(jnp.float32), axis=1).astype(
        jnp.bfloat16
    )
    grid_new = node_update(grid_latent, gsummed, gn_first, gn_second)
    grid_pred = jnp.dot(grid_new, head_full, preferred_element_type=jnp.float32)
    return (mesh_out, edge_out, grid_pred)


def solution(mesh):
    return jax.shard_map(
        body,
        mesh=mesh,
        in_specs=(
            P(("wide", "narrow"), None),
            P(("wide", "narrow"), None),
            P(("wide", "narrow"), None),
            P(("wide", "narrow"), None),
            P(("wide", "narrow"), None),
            P(("wide", "narrow")),
            P(("wide", "narrow"), None),
            P("wide", "narrow", None, None),
            P("wide", "narrow", None, None),
            P("wide", None),
            P("wide", None),
            P("wide", None),
            P("wide", None),
            P("wide", None),
            P("wide", None),
            P("wide", None),
            P("wide", None),
            P("wide", None),
        ),
        out_specs=(
            P(("wide", "narrow"), None),
            P(("wide", "narrow"), None),
            P(("wide", "narrow"), None),
        ),
        check_vma=False,
    )
```

profile of v0, /device:TPU:25, one launch (start us, length us, event | category | flops | bytes accessed | tf_op | source)
XLA Modules:
  0.0 433.1 jit_solution(14685985585206167503)
XLA Ops:
  9.4 10.4 %all_gather.29 = bf16[256,512]{1,0:T(8,128)(2,1)S(1)} all-gather(bf16[64,512]{1,0:T(8,128)(2,1)} %param.18), channel_id=1, replica_groups=mesh['wide'=128,'narrow'=4] {'narrow'}, dimensions={0}, use_global_device_ids=true | all-gather | bytes 327680 | tf_op jit(solution)/shard_map/all_gather | solution.py:129
  20.1 17.3 %gather_fusion = bf16[4096,512]{1,0:T(8,128)(2,1)} fusion(bf16[256,512]{1,0:T(8,128)(2,1)S(1)} %all_gather.29, s32[4096]{0:T(1024)S(1)} %broadcast_clamp_fusion), kind=kCustom, calls=%fused_computation | custom fusion | bytes 8404992 | tf_op jit(solution)/shard_map/jit(_take)/gather | solution.py:130
  37.4 2.6 broadcast_select_fusion
  40.0 2.4 fusion.68
  42.4 19.9 %all-to-all-start = ((bf16[128,1,16,512]{3,2,1,0:T(8,128)(2,1)}), bf16[128,1,16,512]{3,2,1,0:T(8,128)(2,1)S(1)}, u32[]{:S(2)}, u32[]{:S(2)}) async-start(bf16[128,1,16,512]{3,2,1,0:T(8,128)(2,1)} %get-tuple-element.5), calls=%async_computation | async-start | bytes 4194304 | tf_op jit(solution)/shard_map/all_to_all | solution.py:36
  63.8 50.6 %all-to-all-done = bf16[128,1,16,512]{3,2,1,0:T(8,128)(2,1)S(1)} async-done(((bf16[128,1,16,512]{3,2,1,0:T(8,128)(2,1)}), bf16[128,1,16,512]{3,2,1,0:T(8,128)(2,1)S(1)}, u32[]{:S(2)}, u32[]{:S(2)}) %all-to-all-start) | async-done | bytes 2097184 | tf_op jit(solution)/shard_map/all_to_all | solution.py:36
  114.3 9.9 %all-to-all-start.1 = ((bf16[128,1,16,512]{3,2,1,0:T(8,128)(2,1)}), bf16[128,1,16,512]{3,2,1,0:T(8,128)(2,1)}, u32[]{:S(2)}, u32[]{:S(2)}) async-start(bf16[128,1,16,512]{3,2,1,0:T(8,128)(2,1)} %get-tuple-element.6), calls=%async_computation.1 | async-start | bytes 4194304 | tf_op jit(solution)/shard_map/all_to_all | solution.py:36
  125.9 91.0 %all-gather.1 = bf16[128,4,512]{2,1,0:T(4,128)(2,1)S(1)} all-gather(bf16[1,4,512]{2,1,0:T(4,128)(2,1)S(1)} %bitcast.52), channel_id=1, replica_groups=mesh['wide'=128,'narrow'=4] {'wide'}, dimensions={0}, use_global_device_ids=true | all-gather | bytes 528384 | tf_op jit(solution)/shard_map/all_gather | solution.py:109
  217.8 48.4 %all-gather.2 = bf16[128,4,512]{2,1,0:T(4,128)(2,1)S(1)} all-gather(bf16[1,4,512]{2,1,0:T(4,128)(2,1)S(1)} %bitcast.53), channel_id=1, replica_groups=mesh['wide'=128,'narrow'=4] {'wide'}, dimensions={0}, use_global_device_ids=true | all-gather | bytes 528384 | tf_op jit(solution)/shard_map/all_gather | solution.py:111
  267.2 49.5 %all-gather.4 = bf16[128,4,512]{2,1,0:T(4,128)(2,1)S(1)} all-gather(bf16[1,4,512]{2,1,0:T(4,128)(2,1)S(1)} %bitcast.54), channel_id=1, replica_groups=mesh['wide'=128,'narrow'=4] {'wide'}, dimensions={0}, use_global_device_ids=true | all-gather | bytes 528384 | tf_op jit(solution)/shard_map/all_gather | solution.py:113
  317.7 48.6 %all-gather.5 = bf16[128,4,739]{2,1,0:T(4,128)(2,1)S(1)} all-gather(bf16[1,4,739]{2,1,0:T(4,128)(2,1)S(1)} %maximum_bitcast_fusion), channel_id=1, replica_groups=mesh['wide'=128,'narrow'=4] {'wide'}, dimensions={0}, use_global_device_ids=true | all-gather | bytes 762648 | tf_op jit(solution)/shard_map/all_gather | solution.py:10
  366.2 1.3 reshape.337
  367.8 1.2 fusion.27
  369.0 3.8 reshape.327
  374.1 2.2 pad_maximum_fusion
  376.2 5.6 %convolution_convert_fusion = bf16[4352,512]{1,0:T(8,128)(2,1)} fusion(bf16[4096,512]{1,0:T(8,128)(2,1)S(1)} %bitcast.45, bf16[256,512]{1,0:T(8,128)(2,1)S(1)} %all_gather.29, bf16[1536,512]{1,0:T(8,128)(2,1)} %reshape.327), kind=kOutput, calls=%fused_computation.4 | convolution fusion | flops 2292842496 | bytes 9437184 | tf_op jit(solution)/shard_map/dot_general | solution.py:133
  381.8 4.9 %gather_fusion.1 = bf16[512,512]{1,0:T(8,128)(2,1)S(1)} fusion(bf16[4352,512]{1,0:T(8,128)(2,1)} %convolution_convert_fusion, s32[1024]{0:T(1024)S(1)} %pad_clamp_fusion.2), kind=kCustom, calls=%fused_computation.1 | custom fusion | bytes 1050624 | tf_op jit(solution)/shard_map/jit(_take)/gather | solution.py:135
  386.8 2.0 fusion.70
  389.1 1.3 fusion.5
  392.0 3.7 all-to-all-start.2
  395.6 2.1 fusion.19
  397.8 2.5 reshape.333
  400.3 1.5 all-to-all-done.2
  402.6 4.8 %collective-permute-start = (bf16[32,512]{1,0:T(8,128)(2,1)S(1)}, bf16[32,512]{1,0:T(8,128)(2,1)S(1)}, u32[]{:S(2)}, u32[]{:S(2)}) collective-permute-start(bf16[32,512]{1,0:T(8,128)(2,1)S(1)} %get-tuple-element.7), channel_id=1, source_target_pairs={{508,0},{0,4},{4,8},{8,12},{12,16},{16,20},{20,24},{24,28},{28,32}... | collective-permute-start | bytes 98312 | tf_op jit(solution)/shard_map/ppermute | solution.py:53
  407.4 1.9 collective-permute-start.1
  410.0 1.7 add.220
  411.7 2.1 collective-permute-done.1
  413.9 1.4 convolution_convert_fusion.1
  415.2 2.7 gather_fusion.3
  417.9 3.0 fusion.76
  422.2 1.4 reduce_sum.100
  423.6 1.7 fusion.79
  (106 shorter events, 15.5 us)
Async XLA Ops:
  7.2 360.6 %all-gather.11.cloned.1.call-start = ((), (), s32[]{:S(2)}) async-start(), calls=%async_computation.3 | async-start | bytes 1056768 | tf_op jit(solution)/shard_map/all_gather | solution.py:110
  42.4 71.9 %all-to-all-start = ((bf16[128,1,16,512]{3,2,1,0:T(8,128)(2,1)}), bf16[128,1,16,512]{3,2,1,0:T(8,128)(2,1)S(1)}, u32[]{:S(2)}, u32[]{:S(2)}) async-start(bf16[128,1,16,512]{3,2,1,0:T(8,128)(2,1)} %get-tuple-element.5), calls=%async_computation | async-start | bytes 4194304 | tf_op jit(solution)/shard_map/all_to_all | solution.py:36
  62.3 306.7 %all-gather.15.cloned.1.call-start = ((), (), s32[]{:S(2)}) async-start(), calls=%async_computation.5 | async-start | bytes 2113536 | tf_op jit(solution)/shard_map/all_gather | solution.py:108
  63.0 332.6 %all-gather.13.cloned.1.call-start = ((), (), s32[]{:S(2)}) async-start(), calls=%async_computation.4 | async-start | bytes 1056768 | tf_op jit(solution)/shard_map/all_gather | solution.py:114
  114.3 10.5 %copy-start.14 = (s32[64,8]{0,1:T(8,128)S(1)}, s32[64,8]{0,1:T(8,128)}, u32[]{:S(2)}) copy-start(s32[64,8]{0,1:T(8,128)} %param.22) | copy-start | bytes 6148
  114.3 10.8 %copy-start.19 = (s32[1,1,2,32]{3,2,1,0:T(2,128)S(1)}, s32[1,1,2,32]{3,2,1,0:T(2,128)}, u32[]{:S(2)}) copy-start(s32[1,1,2,32]{3,2,1,0:T(2,128)} %param.26) | copy-start | bytes 772
  114.3 10.9 %copy-start.15 = (s32[256,3]{0,1:T(4,128)S(1)}, s32[256,3]{0,1:T(4,128)}, u32[]{:S(2)}) copy-start(s32[256,3]{0,1:T(4,128)} %param.24) | copy-start | bytes 9220
  114.3 11.5 %copy-start.11 = (bf16[4,512]{1,0:T(4,128)(2,1)S(1)}, bf16[4,512]{1,0:T(4,128)(2,1)}, u32[]{:S(2)}) copy-start(bf16[4,512]{1,0:T(4,128)(2,1)} %param.28) | copy-start | bytes 12292
  114.3 259.7 %all-to-all-start.1 = ((bf16[128,1,16,512]{3,2,1,0:T(8,128)(2,1)}), bf16[128,1,16,512]{3,2,1,0:T(8,128)(2,1)}, u32[]{:S(2)}, u32[]{:S(2)}) async-start(bf16[128,1,16,512]{3,2,1,0:T(8,128)(2,1)} %get-tuple-element.6), calls=%async_computation.1 | async-start | bytes 4194304 | tf_op jit(solution)/shard_map/all_to_all | solution.py:36
  124.2 93.6 %copy-start.12 = (bf16[4,512]{1,0:T(4,128)(2,1)S(1)}, bf16[4,512]{1,0:T(4,128)(2,1)}, u32[]{:S(2)}) copy-start(bf16[4,512]{1,0:T(4,128)(2,1)} %param.30) | copy-start | bytes 12292
  124.2 273.5 %all-gather.17.cloned.1.call-start = ((), (), s32[]{:S(2)}) async-start(), calls=%async_computation.6 | async-start | bytes 2113536 | tf_op jit(solution)/shard_map/all_gather | solution.py:112
  125.8 141.3 %copy-start.13 = (bf16[4,512]{1,0:T(4,128)(2,1)S(1)}, bf16[4,512]{1,0:T(4,128)(2,1)}, u32[]{:S(2)}) copy-start(bf16[4,512]{1,0:T(4,128)(2,1)} %param.32) | copy-start | bytes 12292
  217.8 99.8 %copy-start.16 = (bf16[4,512]{1,0:T(4,128)(2,1)S(1)}, bf16[4,512]{1,0:T(4,128)(2,1)}, u32[]{:S(2)}) copy-start(bf16[4,512]{1,0:T(4,128)(2,1)} %param.34) | copy-start | bytes 12292
  217.8 99.8 %copy-start.17 = (bf16[4,227]{1,0:T(4,128)(2,1)S(1)}, bf16[4,227]{1,0:T(4,128)(2,1)}, u32[]{:S(2)}) copy-start(bf16[4,227]{1,0:T(4,128)(2,1)} %param.35) | copy-start | bytes 5452
  316.7 50.9 %copy-start.18 = (s32[64]{0:T(128)S(1)}, s32[64]{0:T(128)}, u32[]{:S(2)}) copy-start(s32[64]{0:T(128)} %param.23) | copy-start | bytes 772
  316.7 51.0 %copy-start.3 = (bf16[64,512]{1,0:T(8,128)(2,1)S(1)}, bf16[64,512]{1,0:T(8,128)(2,1)}, u32[]{:S(2)}) copy-start(bf16[64,512]{1,0:T(8,128)(2,1)} %param.18) | copy-start | bytes 196612
  381.8 4.9 %copy-start.7 = (bf16[512,512]{1,0:T(8,128)(2,1)S(1)}, bf16[512,512]{1,0:T(8,128)(2,1)}, u32[]{:S(2)}) copy-start(bf16[512,512]{1,0:T(8,128)(2,1)} %reshape.329) | copy-start | bytes 1572868
  381.8 5.0 %copy-start.8 = (bf16[512,512]{1,0:T(8,128)(2,1)S(1)}, bf16[512,512]{1,0:T(8,128)(2,1)}, u32[]{:S(2)}) copy-start(bf16[512,512]{1,0:T(8,128)(2,1)} %param.19) | copy-start | bytes 1572868
  388.8 1.6 copy-start.5
  388.8 1.6 copy-start.9
  390.4 5.3 %copy-start.1 = (bf16[256,512]{1,0:T(8,128)(2,1)S(1)}, bf16[256,512]{1,0:T(8,128)(2,1)}, u32[]{:S(2)}) copy-start(bf16[256,512]{1,0:T(8,128)(2,1)} %param.20) | copy-start | bytes 786436
  391.2 9.1 %copy-start.10 = (bf16[64,512]{1,0:T(8,128)(2,1)}, bf16[64,512]{1,0:T(8,128)(2,1)S(1)}, u32[]{:S(2)}) copy-start(bf16[64,512]{1,0:T(8,128)(2,1)S(1)} %add_convert_fusion.4) | copy-start | bytes 196612
  392.0 9.8 %all-to-all-start.2 = ((bf16[4,64,512]{2,1,0:T(8,128)(2,1)}), bf16[4,64,512]{2,1,0:T(8,128)(2,1)S(1)}, u32[]{:S(2)}, u32[]{:S(2)}) async-start(bf16[4,64,512]{2,1,0:T(8,128)(2,1)} %broadcast_in_dim.60), calls=%async_computation.2 | async-start | bytes 524288 | tf_op jit(solution)/shard_map/all_to_all | solution.py:42
  400.3 9.1 %copy-start = (bf16[1536,512]{1,0:T(8,128)(2,1)}, bf16[1536,512]{1,0:T(8,128)(2,1)S(1)}, u32[]{:S(2)}) copy-start(bf16[1536,512]{1,0:T(8,128)(2,1)S(1)} %reshape.333) | copy-start | bytes 4718596
  402.6 9.2 %collective-permute-start = (bf16[32,512]{1,0:T(8,128)(2,1)S(1)}, bf16[32,512]{1,0:T(8,128)(2,1)S(1)}, u32[]{:S(2)}, u32[]{:S(2)}) collective-permute-start(bf16[32,512]{1,0:T(8,128)(2,1)S(1)} %get-tuple-element.7), channel_id=1, source_target_pairs={{508,0},{0,4},{4,8},{8,12},{12,16},{16,20},{20,24},{24,28},{28,32}... | collective-permute-start | bytes 98312 | tf_op jit(solution)/shard_map/ppermute | solution.py:53
  407.4 6.4 %collective-permute-start.1 = (bf16[32,512]{1,0:T(8,128)(2,1)S(1)}, bf16[32,512]{1,0:T(8,128)(2,1)S(1)}, u32[]{:S(2)}, u32[]{:S(2)}) collective-permute-start(bf16[32,512]{1,0:T(8,128)(2,1)S(1)} %get-tuple-element.8), channel_id=1, source_target_pairs={{4,0},{8,4},{12,8},{16,12},{20,16},{24,20},{28,24},{32,28},{36,32}... | collective-permute-start | bytes 98312 | tf_op jit(solution)/shard_map/ppermute | solution.py:53
  415.2 2.7 copy-start.4
  421.7 1.9 copy-start.2
  421.7 1.9 copy-start.6
Sparse Core Ops, SparseCore 0:
  11.0 116.4 all-gather.10
  130.6 97.4 all-gather.14
  231.1 75.0 all-gather.12
  309.2 79.7 all-gather.16
where the time goes:
time: 434 us; the launch traced here: 433 us
  blocking collectives  248 us (57%)
  waiting for transfers between devices  56.8 us (13%)
  local copies, waits for them, and re-layouts  43.8 us (10%)
  starting transfers between devices  40.3 us (9%)
  matrix products  20.1 us (5%)
  between operations  14.3 us (3%)
  other arithmetic  9.9 us (2%)
    all_gather x1, blocking collectives, body(): lax.all_gather(proc_edge_out, 'wide', axis=0, tiled=True)  91 us
    all_to_all x2, waiting for transfers between devices, several_exchanges(): lax.all_to_all(share, axis, split_axis=0, concat_axis=0, tiled=True)  50.6 us
    all_gather x1, blocking collectives, body(): lax.all_gather(dec_edge_out, 'wide', axis=0, tiled=True)  49.5 us
    all_gather x1, blocking collectives, sent_together(): whole = lax.all_gather(both, axis, axis=dim, tiled=True)  48.6 us
    all_gather x1, blocking collectives, body(): lax.all_gather(proc_node_out, 'wide', axis=0, tiled=True)  48.4 us
    all_to_all x2, starting transfers between devices, several_exchanges(): lax.all_to_all(share, axis, split_axis=0, concat_axis=0, tiled=True)  29.7 us
    gather x1, local copies, waits for them, and re-layouts, body(): jnp.take(patch, mesh_send_rows.reshape(-1), axis=0)  17.3 us
    unnamed x49, local copies, waits for them, and re-layouts  11.5 us
  transfers between devices with their start and end apart: 9, of which 3 were waited for; matrix products, arithmetic and copies ran while one was open for 14% of the time, Pallas kernels for 0%

commit v1 on v0

v1 whole, which is shorter than its diff:
```python
import jax
import jax.numpy as jnp
from jax import lax
from jax.experimental import pallas as pl
from jax.experimental.pallas import tpu as pltpu
from jax.sharding import PartitionSpec as P

BF16 = jnp.bfloat16
F32 = jnp.float32
CAPACITY = 192


def matmul(a, b):
    return jnp.dot(a, b, preferred_element_type=F32)


def second_layer(pre, w_second):
    active = (pre / (1.0 + jnp.exp(-pre))).astype(BF16)
    values = matmul(active, w_second)
    center = values - jnp.mean(values, axis=-1, keepdims=True)
    spread = jnp.mean(center * center, axis=-1, keepdims=True)
    return center * lax.rsqrt(spread + 1e-05)


def marks(hit):
    return jnp.where(hit, 1.0, 0.0).astype(BF16)


def selection(index, size):
    columns = lax.broadcasted_iota(jnp.int32, (index.shape[0], size), 1)
    return marks(index == columns)


def pack_kernel(*refs):
    *pieces, out, stage = refs
    stage[...] = jnp.zeros_like(stage)
    first = 0
    for piece in pieces:
        rows, columns = piece.shape
        stage[first : first + rows, 0:columns] = piece[...].astype(F32)
        first += rows
    out[...] = stage[...].astype(BF16)


def packed(pieces, rows, width):
    return pl.pallas_call(
        pack_kernel,
        out_shape=jax.ShapeDtypeStruct((rows, width), BF16),
        scratch_shapes=[pltpu.VMEM((rows, width), F32)],
        name="pack",
    )(*pieces)


def processor_kernel(
    place, live, got, extra, edges, near, latent, w_first, w_second, n_first, n_second, edge_out, mesh_out, messages
):
    step, steps = pl.program_id(0), pl.num_programs(0)
    width = edges.shape[1]
    rows = matmul(selection(place[...], got.shape[0]), got[...]) + extra[...].astype(F32)
    sent = matmul(rows.astype(BF16), w_first[width : 2 * width]).astype(BF16)
    receiver = matmul(near[...], w_first[2 * width :])
    count = receiver.shape[0]
    spread = jnp.broadcast_to(receiver[:, None, :], (count, edges.shape[0] // count, width))
    pre = matmul(edges[...], w_first[:width]) + sent.astype(F32) + spread.reshape(edges.shape)
    updated = (edges[...].astype(F32) + second_layer(pre, w_second[...])).astype(BF16)
    edge_out[...] = updated
    kept = (updated.astype(F32) * live[...]).reshape(spread.shape)
    messages[pl.ds(pl.multiple_of(step * count, count), count)] = jnp.sum(kept, axis=1).astype(BF16)

    @pl.when(step == steps - 1)
    def _():
        node_pre = matmul(latent[...], n_first[:width]) + matmul(messages[...], n_first[width:])
        mesh_out[...] = (latent[...].astype(F32) + second_layer(node_pre, n_second[...])).astype(BF16)


def processor(place, live, got, extra, edges, latent, w_first, w_second, n_first, n_second, steps=4):
    slots, width = edges.shape
    nodes = latent.shape[0]

    def tiles(array):
        return pl.BlockSpec((array.shape[0] // steps, array.shape[1]), lambda i: (i, 0))

    def whole(array):
        return pl.BlockSpec(array.shape, lambda i: (0, 0))

    return pl.pallas_call(
        processor_kernel,
        grid=(steps,),
        in_specs=[tiles(place), tiles(live), whole(got), tiles(extra), tiles(edges), tiles(latent), whole(latent)]
        + [whole(w) for w in (w_first, w_second, n_first, n_second)],
        out_specs=[tiles(edges), whole(latent)],
        out_shape=[jax.ShapeDtypeStruct(edges.shape, BF16), jax.ShapeDtypeStruct(latent.shape, BF16)],
        scratch_shapes=[pltpu.VMEM((nodes, width), BF16)],
        cost_estimate=pl.CostEstimate(flops=2_000_000_000, bytes_accessed=8_000_000, transcendentals=600_000),
        name="processor",
    )(place, live, got, extra, edges, latent, latent, w_first, w_second, n_first, n_second)


def decoder_kernel(
    named, index, near_a, near_b, edges, latent, w_first, w_second, n_first, n_second, head, out, sent
):
    width = edges.shape[1]

    @pl.when(pl.program_id(0) == 0)
    def _():
        columns = near_a.shape[0]
        table = matmul(selection(named[...], columns), near_a[...])
        table = table + matmul(selection(named[...] - columns, columns), near_b[...])
        sent[...] = matmul(table.astype(BF16), w_first[width : 2 * width]).astype(BF16)

    count, points = edges.shape[0], latent.shape[0]
    fanin = count // points
    offset = lax.broadcasted_iota(jnp.int32, (count, points), 0) - fanin * lax.broadcasted_iota(
        jnp.int32, (count, points), 1
    )
    onto = lax.broadcasted_iota(jnp.int32, (points, count), 1) - fanin * lax.broadcasted_iota(
        jnp.int32, (points, count), 0
    )
    receivers = matmul(marks((offset >= 0) & (offset < fanin)), latent[...]).astype(BF16)
    pre = matmul(edges[...], w_first[:width]) + matmul(receivers, w_first[2 * width :])
    pre = pre + matmul(selection(index[...], sent.shape[0]), sent[...])
    updated = (edges[...].astype(F32) + second_layer(pre, w_second[...])).astype(BF16)
    summed = matmul(marks((onto >= 0) & (onto < fanin)), updated).astype(BF16)
    point_pre = matmul(latent[...], n_first[:width]) + matmul(summed, n_first[width:])
    point_new = (latent[...].astype(F32) + second_layer(point_pre, n_second[...])).astype(BF16)
    out[...] = matmul(point_new, head[...])


def decoder(named, index, near_a, near_b, edges, latent, w_first, w_second, n_first, n_second, head, steps=2):
    width = edges.shape[1]

    def tiles(array):
        return pl.BlockSpec((array.shape[0] // steps, array.shape[1]), lambda i: (i, 0))

    def whole(array):
        return pl.BlockSpec(array.shape, lambda i: (0, 0))

    out = jax.ShapeDtypeStruct((latent.shape[0], head.shape[1]), F32)
    return pl.pallas_call(
        decoder_kernel,
        grid=(steps,),
        in_specs=[whole(named), tiles(index), whole(near_a), whole(near_b), tiles(edges), tiles(latent)]
        + [whole(w) for w in (w_first, w_second, n_first, n_second, head)],
        out_specs=tiles(out),
        out_shape=out,
        scratch_shapes=[pltpu.VMEM((named.shape[0], width), BF16)],
        cost_estimate=pl.CostEstimate(flops=3_000_000_000, bytes_accessed=8_000_000, transcendentals=1_000_000),
        name="decoder",
    )(named, index, near_a, near_b, edges, latent, w_first, w_second, n_first, n_second, head)


def exchanged(blocks, axis):
    return lax.all_to_all(blocks, axis, split_axis=0, concat_axis=0, tiled=True)


def passed_along(block, axis, distance):
    count = lax.axis_size(axis)
    return lax.ppermute(block, axis, [((i - distance) % count, i) for i in range(count)])


def one_hot(index, size):
    return (index[:, None] == lax.broadcasted_iota(jnp.int32, (1, size), 1)).astype(BF16)


def wanted_rows(senders, send_rows, nodes):
    peers, send = send_rows.shape
    group = lax.axis_size("narrow")
    patch = nodes * group
    slots = senders.reshape(-1)
    incoming = exchanged(send_rows, "wide")
    halo = jnp.maximum(slots - patch, 0)
    lists = matmul(one_hot(halo // send, peers), incoming.astype(BF16))
    column = lax.broadcasted_iota(jnp.int32, (1, send), 1)
    remote = jnp.sum(jnp.where((halo % send)[:, None] == column, lists, 0.0), axis=1)
    own = slots < patch
    row = jnp.where(own, slots, remote.astype(jnp.int32))
    source = jnp.where(own, lax.axis_index("wide"), halo // send)
    return row // nodes, source, row % nodes


def ranks_within(owner, group):
    mine = one_hot(owner, group)
    count = owner.shape[0]
    before = lax.broadcasted_iota(jnp.int32, (count, count), 0) > lax.broadcasted_iota(
        jnp.int32, (count, count), 1
    )
    earlier = matmul(before.astype(BF16), mine)
    rank = jnp.sum(earlier * mine.astype(F32), axis=1).astype(jnp.int32)
    most = jnp.max(jnp.sum(mine.astype(F32), axis=0))
    return rank, most


def requests(select, source, local, stride, capacity, most):
    group = lax.axis_size("narrow")
    asked = matmul(jnp.stack([source, local], axis=0).astype(BF16), select).astype(jnp.int32)
    ids = (asked[0] * stride + asked[1]).reshape(group, capacity)
    ids = jnp.pad(ids, ((0, 0), (0, -capacity % 128 + 128)))
    lane = lax.broadcasted_iota(jnp.int32, (1, ids.shape[1]), 1)
    here = exchanged(jnp.where(lane == capacity, most, ids), "narrow")
    return here[:, :capacity].reshape(-1), jnp.max(here[:, capacity])


def places(owner, rank, first, capacity):
    here = rank - first
    return jnp.where((here >= 0) & (here < capacity), owner * capacity + here, -1)


def rows_of(table, ids):
    return table.at[ids].get(mode="promise_in_bounds")


def delivered(found):
    width = found.shape[1]
    return exchanged(found.reshape(lax.axis_size("narrow"), -1, width), "narrow").reshape(-1, width)


def all_devices_max(value):
    copies = jnp.broadcast_to(value, (lax.axis_size("wide"), 8))
    return jnp.max(exchanged(copies, "wide"))


def two_patches(block, first):
    group, peers = lax.axis_size("narrow"), lax.axis_size("wide")
    count = group * peers
    members = [
        [(2 * group * k + first * group + j) % count for j in range(2 * group)] for k in range(peers // 2)
    ]
    copies = jnp.broadcast_to(block, (2 * group, *block.shape))
    got = lax.all_to_all(
        copies, ("wide", "narrow"), split_axis=0, concat_axis=0, axis_index_groups=members, tiled=True
    )
    return got.reshape(-1, block.shape[1])


def body(
    mesh_latent,
    mesh_edges,
    grid_latent,
    decoder_edges,
    mesh_senders,
    mesh_degree,
    decoder_senders,
    mesh_send_rows,
    decoder_send_rows,
    proc_edge_in,
    proc_edge_out,
    proc_node_in,
    proc_node_out,
    dec_edge_in,
    dec_edge_out,
    grid_node_in,
    grid_node_out,
    output_head,
):
    nodes, width = mesh_latent.shape
    degree = mesh_senders.shape[1]
    slots = nodes * degree
    channels = output_head.shape[1]
    pieces = (mesh_latent, proc_edge_in, proc_edge_out, proc_node_in, proc_node_out, output_head)
    pieces = pieces + (dec_edge_in, dec_edge_out, grid_node_in, grid_node_out)
    pack = packed(pieces, 2 * nodes, width)
    stride = pack.shape[0]
    table = lax.all_gather(pack, "wide", axis=0, tiled=True)

    def weight(gathered, first, count):
        parts = gathered.reshape(-1, stride, width)
        return parts[:, nodes + first : nodes + first + count].reshape(-1, width)

    owner, source, local = wanted_rows(mesh_senders, mesh_send_rows[0, 0], nodes)
    rank, most = ranks_within(owner, lax.axis_size("narrow"))
    group = lax.axis_size("narrow")
    place = places(owner, rank, 0, CAPACITY)
    ids, most = requests(one_hot(place, group * CAPACITY), source, local, stride, CAPACITY, most.astype(jnp.int32))
    most = all_devices_max(most)
    lists = decoder_send_rows[0, 0]
    odd = lax.axis_index("wide") % 2
    span = nodes * group
    named = jnp.concatenate(
        [
            odd * span + jnp.arange(span, dtype=jnp.int32),
            (1 - odd) * 2 * span + passed_along(lists[0], "wide", 1),
            (1 + 2 * odd) * span + passed_along(lists[1], "wide", -1),
        ]
    )
    live = lax.broadcasted_iota(jnp.int32, (nodes, degree), 1) < mesh_degree[:, None]
    place, live, named, index, ids = lax.optimization_barrier(
        (
            place.reshape(-1, 1),
            live.astype(F32).reshape(-1, 1),
            named.reshape(-1, 1),
            decoder_senders.reshape(-1, 1),
            ids,
        )
    )
    found = rows_of(table, ids)
    got = delivered(found)
    most, _ = lax.optimization_barrier((most, found))

    def fetch_rest():
        rest = slots - CAPACITY
        late = one_hot(places(owner, rank, CAPACITY, rest), group * rest)
        late_ids, _ = requests(late, source, local, stride, rest, most)
        return matmul(late, delivered(rows_of(table, late_ids))).astype(BF16)

    extra = lax.cond(most > CAPACITY, fetch_rest, lambda: jnp.zeros((slots, width), BF16))
    edge_out, mesh_out = processor(
        place,
        live,
        got,
        extra,
        mesh_edges,
        mesh_latent,
        weight(table, 0, 12),
        weight(table, 12, 4),
        weight(table, 16, 8),
        weight(table, 24, 4),
    )

    late_table, _ = lax.optimization_barrier((table, mesh_out))
    grid_pred = decoder(
        named,
        index,
        two_patches(mesh_out, 0),
        two_patches(mesh_out, 1),
        decoder_edges,
        grid_latent,
        weight(late_table, 32, 12),
        weight(late_table, 44, 4),
        weight(late_table, 48, 8),
        weight(late_table, 56, 4),
        weight(late_table, 28, 4)[:, :channels],
    )
    return (mesh_out, edge_out, grid_pred)


def solution(mesh):
    rows = P(("wide", "narrow"), None)
    lists = P("wide", "narrow", None, None)
    return jax.shard_map(
        body,
        mesh=mesh,
        in_specs=(rows,) * 5 + (P(("wide", "narrow")), rows, lists, lists) + (P("wide", None),) * 9,
        out_specs=(rows,) * 3,
        check_vma=False,
    )
```

time: 434 us -> 210 us (0.48)
  the two profiles are of different devices: /device:TPU:25 before, /device:TPU:2 now
where the time goes in v1:
time: 210 us; the launch traced here: 209 us
  waiting for transfers between devices  57.9 us (28%)
  starting transfers between devices  51.3 us (24%)
  local copies, waits for them, and re-layouts  45.7 us (22%)
  Pallas kernels  19.1 us (9%)
  between operations  15.6 us (7%)
  blocking collectives  14.1 us (7%)
  other arithmetic  4.08 us (2%)
    all_gather x1, waiting for transfers between devices, body(): table = lax.all_gather(pack, 'wide', axis=0, tiled=True)  39.4 us
    all_to_all x4, starting transfers between devices, exchanged(): return lax.all_to_all(blocks, axis, split_axis=0, concat_axis=0, tiled=True)  34.3 us
    all_to_all x4, waiting for transfers between devices, exchanged(): return lax.all_to_all(blocks, axis, split_axis=0, concat_axis=0, tiled=True)  15.2 us
    all_to_all x1, blocking collectives, two_patches(): lax.all_to_all(copies, ('wide', 'narrow'), split_axis=0, concat_axis=0, a...  14.1 us
    gather x1, local copies, waits for them, and re-layouts, rows_of(): return table.at[ids].get(mode='promise_in_bounds')  11.3 us
    reshape x9, local copies, waits for them, and re-layouts, weight(): return parts[:, nodes + first:nodes + first + count].reshape(-1, width)  11 us
    pallas_call x1, Pallas kernels, decoder(): pl.pallas_call(decoder_kernel, grid=(steps,), in_specs=[whole(named), til...  9.01 us
    ppermute x2, starting transfers between devices, passed_along(): lax.ppermute(block, axis, [((i - distance) % count, i) for i in range(cou...  8.74 us
  transfers between devices with their start and end apart: 8, of which 5 were waited for; matrix products, arithmetic and copies ran while one was open for 16% of the time, Pallas kernels for 0%

profile of v1, /device:TPU:2, one launch (start us, length us, event | category | flops | bytes accessed | tf_op | source)
XLA Modules:
  0.0 209.0 jit_solution(10543066137184123861)
XLA Ops:
  7.2 1.6 pack.1
  8.8 1.4 copy.86
  10.3 17.8 %all-to-all-start.2 = ((s32[128,1,32]{2,1,0:T(1,128)}), s32[128,1,32]{2,1,0:T(1,128)S(1)}, u32[]{:S(2)}, u32[]{:S(2)}) async-start(s32[128,1,32]{2,1,0:T(1,128)} %bitcast.2), calls=%async_computation.2 | async-start | bytes 131072 | tf_op jit(solution)/shard_map/all_to_all | solution.py:153
  28.9 6.8 %collective-permute-start.1 = (s32[32]{0:T(128)S(1)}, s32[32]{0:T(128)S(1)}, u32[]{:S(2)}, u32[]{:S(2)}) collective-permute-start(s32[32]{0:T(128)S(1)} %get-tuple-element.145), channel_id=1, source_target_pairs={{4,0},{8,4},{12,8},{16,12},{20,16},{24,20},{28,24},{32,28},{36,32}... | collective-permute-start | bytes 392 | tf_op jit(solution)/shard_map/ppermute | solution.py:158
  35.7 1.9 collective-permute-start
  40.7 3.2 %collective-permute-done = s32[32]{0:T(128)S(1)} collective-permute-done((s32[32]{0:T(128)S(1)}, s32[32]{0:T(128)S(1)}, u32[]{:S(2)}, u32[]{:S(2)}) %collective-permute-start) | collective-permute-done | bytes 160 | tf_op jit(solution)/shard_map/ppermute | solution.py:158
  47.6 4.8 %all-to-all-start.3 = ((s32[4,1,384]{2,1,0:T(1,128)}), s32[4,1,384]{2,1,0:T(1,128)S(1)}, u32[]{:S(2)}, u32[]{:S(2)}) async-start(s32[4,1,384]{2,1,0:T(1,128)} %all_to_all.40), calls=%async_computation.3 | async-start | bytes 12288 | tf_op jit(solution)/shard_map/all_to_all | solution.py:153
  52.4 0.9 fusion.29.place
  53.3 2.9 %all-to-all-done.3 = s32[4,1,384]{2,1,0:T(1,128)S(1)} async-done(((s32[4,1,384]{2,1,0:T(1,128)}), s32[4,1,384]{2,1,0:T(1,128)S(1)}, u32[]{:S(2)}, u32[]{:S(2)}) %all-to-all-start.3) | async-done | bytes 6176 | tf_op jit(solution)/shard_map/all_to_all | solution.py:153
  57.1 1.3 broadcast_in_dim.62
  58.3 7.0 %all-to-all-start.5 = ((s32[128,1,8]{2,1,0:T(1,128)}), s32[128,1,8]{2,1,0:T(1,128)S(1)}, u32[]{:S(2)}, u32[]{:S(2)}) async-start(s32[128,1,8]{2,1,0:T(1,128)} %broadcast_in_dim.62), calls=%async_computation.5 | async-start | bytes 131072 | tf_op jit(solution)/shard_map/all_to_all | solution.py:153
  65.3 11.1 %all-to-all-done.5 = s32[128,1,8]{2,1,0:T(1,128)S(1)} async-done(((s32[128,1,8]{2,1,0:T(1,128)}), s32[128,1,8]{2,1,0:T(1,128)S(1)}, u32[]{:S(2)}, u32[]{:S(2)}) %all-to-all-start.5) | async-done | bytes 4128 | tf_op jit(solution)/shard_map/all_to_all | solution.py:153
  77.2 39.4 %all-gather.2.cloned.1.call-done = bf16[16384,512]{1,0:T(8,128)(2,1)} async-done(((bf16[128,512]{1,0:T(8,128)(2,1)}), bf16[16384,512]{1,0:T(8,128)(2,1)}) %all-gather.2.cloned.1.call-update) | async-done | bytes 16777232 | tf_op jit(solution)/shard_map/all_gather | solution.py:263
  116.6 11.3 %gather_fusion.1 = bf16[768,512]{1,0:T(8,128)(2,1)} fusion(bf16[16384,512]{1,0:T(8,128)(2,1)} %all-gather.2.cloned.1.call-done, s32[1024]{0:T(1024)S(1)} %pad_clamp_fusion.1), kind=kCustom, calls=%fused_computation.1 | custom fusion | bytes 1575936 | tf_op jit(solution)/shard_map/gather | solution.py:209
  128.8 4.7 %all-to-all-start.4 = ((bf16[4,192,512]{2,1,0:T(8,128)(2,1)}), bf16[4,192,512]{2,1,0:T(8,128)(2,1)S(1)}, u32[]{:S(2)}, u32[]{:S(2)}) async-start(bf16[4,192,512]{2,1,0:T(8,128)(2,1)} %bitcast.9), calls=%async_computation.4 | async-start | bytes 1572864 | tf_op jit(solution)/shard_map/all_to_all | solution.py:153
  134.4 1.8 slice.86
  136.2 1.4 reshape.420.w_first
  137.6 2.0 fusion.51
  139.5 0.9 reshape.421.w_second
  141.4 2.3 %slice_bitcast_fusion.1.n_first = bf16[1024,512]{1,0:T(8,128)(2,1)} fusion(bf16[128,128,512]{2,1,0:T(8,128)(2,1)} %bitcast.32), kind=kLoop, calls=%fused_computation.46 | loop fusion | bytes 2097152 | tf_op jit(solution)/shard_map/reshape | solution.py:267
  143.6 1.2 all-to-all-done.4
  145.7 8.5 %processor.1 = (bf16[512,512]{1,0:T(8,128)(2,1)}, bf16[64,512]{1,0:T(8,128)(2,1)}) custom-call(s32[512,1]{1,0:T(8,128)} %fusion.29.place, f32[512,1]{1,0:T(8,128)} %copy.98.live, bf16[768,512]{1,0:T(8,128)(2,1)} %bitcast.38, bf16[512,512]{1,0:T(8,128)(2,1)S(1)} %get-tuple-element.148.extra, bf16[512,512]{1,0:T(8,128)(2,1)} %edges.2, bf16[64,512]{1,0:T(8,128)(2,1)} %latent.2, ...), custom_call_target="tpu_custom_call" | custom-call | flops 2000000000 | bytes 8000000 | tf_op jit(solution)/shard_map/processor/pallas_call | solution.py:86
  154.2 1.7 broadcast_in_dim.63
  155.9 14.1 %all_to_all.57 = bf16[8,64,512]{2,1,0:T(8,128)(2,1)} all-to-all(bf16[8,64,512]{2,1,0:T(8,128)(2,1)} %broadcast_in_dim.63), channel_id=1, replica_groups={{0,1,2,3,4,5,6,7},{8,9,10,11,12,13,14,15},{16,17,18,19,20,21,22,23},{24..., dimensions={0} | all-to-all | bytes 1048576 | tf_op jit(solution)/shard_map/all_to_all | solution.py:229
  170.0 8.2 %all-to-all-start.7 = ((bf16[8,64,512]{2,1,0:T(8,128)(2,1)}), bf16[8,64,512]{2,1,0:T(8,128)(2,1)S(1)}, u32[]{:S(2)}, u32[]{:S(2)}) async-start(bf16[8,64,512]{2,1,0:T(8,128)(2,1)} %broadcast_in_dim.63), calls=%async_computation.7 | async-start | bytes 1048576 | tf_op jit(solution)/shard_map/all_to_all | solution.py:229
  179.0 1.0 copy.100.index
  180.0 1.8 slice.90
  181.7 1.4 reshape.427.w_first
  183.1 2.5 %fusion.50 = (bf16[128,4,512]{2,1,0:T(4,128)(2,1)S(1)}, bf16[128,4,512]{2,1,0:T(4,128)(2,1)S(1)}, bf16[128,4,512]{2,1,0:T(4,128)(2,1)S(1)}) fusion(bf16[128,128,512]{2,1,0:T(8,128)(2,1)} %bitcast.34), kind=kLoop, calls=%fused_computation.117 | loop fusion | bytes 3145728 | tf_op jit(solution)/shard_map/slice | solution.py:267
  188.3 2.3 %slice_bitcast_fusion.n_first = bf16[1024,512]{1,0:T(8,128)(2,1)} fusion(bf16[128,128,512]{2,1,0:T(8,128)(2,1)} %bitcast.35), kind=kLoop, calls=%fused_computation.45 | loop fusion | bytes 2097152 | tf_op jit(solution)/shard_map/reshape | solution.py:267
  191.4 9.0 %decoder.1 = f32[256,227]{1,0:T(8,128)} custom-call(s32[320,1]{1,0:T(8,128)} %copy.99.named, s32[768,1]{1,0:T(8,128)} %copy.100.index, bf16[512,512]{1,0:T(8,128)(2,1)} %bitcast.39, bf16[512,512]{1,0:T(8,128)(2,1)} %bitcast.40, bf16[768,512]{1,0:T(8,128)(2,1)} %edges.3, bf16[256,512]{1,0:T(8,128)(2,1)} %latent.3, bf16[1536,512]{1,0:T(8,128)(2,1)} %reshape.427.w_first, ...), custom_call_target="tpu_custom_call" | custom-call | flops 3000000000 | bytes 8000000 | tf_op jit(solution)/shard_map/decoder/pallas_call | solution.py:139
  200.4 1.8 copy.101
  (63 shorter events, 15.6 us)
Async XLA Ops:
  7.2 109.4 %all-gather.2.cloned.1.call-start = ((), (), s32[]{:S(2)}) async-start(), calls=%async_computation.8 | async-start | bytes 16908288 | tf_op jit(solution)/shard_map/all_gather | solution.py:263
  10.3 33.7 %all-to-all-start.2 = ((s32[128,1,32]{2,1,0:T(1,128)}), s32[128,1,32]{2,1,0:T(1,128)S(1)}, u32[]{:S(2)}, u32[]{:S(2)}) async-start(s32[128,1,32]{2,1,0:T(1,128)} %bitcast.2), calls=%async_computation.2 | async-start | bytes 131072 | tf_op jit(solution)/shard_map/all_to_all | solution.py:153
  28.9 11.8 %collective-permute-start.1 = (s32[32]{0:T(128)S(1)}, s32[32]{0:T(128)S(1)}, u32[]{:S(2)}, u32[]{:S(2)}) collective-permute-start(s32[32]{0:T(128)S(1)} %get-tuple-element.145), channel_id=1, source_target_pairs={{4,0},{8,4},{12,8},{16,12},{20,16},{24,20},{28,24},{32,28},{36,32}... | collective-permute-start | bytes 392 | tf_op jit(solution)/shard_map/ppermute | solution.py:158
  35.7 8.2 %collective-permute-start = (s32[32]{0:T(128)S(1)}, s32[32]{0:T(128)S(1)}, u32[]{:S(2)}, u32[]{:S(2)}) collective-permute-start(s32[32]{0:T(128)S(1)} %get-tuple-element.144), channel_id=1, source_target_pairs={{508,0},{0,4},{4,8},{8,12},{12,16},{16,20},{20,24},{24,28},{28,32}... | collective-permute-start | bytes 392 | tf_op jit(solution)/shard_map/ppermute | solution.py:158
  47.6 8.7 %all-to-all-start.3 = ((s32[4,1,384]{2,1,0:T(1,128)}), s32[4,1,384]{2,1,0:T(1,128)S(1)}, u32[]{:S(2)}, u32[]{:S(2)}) async-start(s32[4,1,384]{2,1,0:T(1,128)} %all_to_all.40), calls=%async_computation.3 | async-start | bytes 12288 | tf_op jit(solution)/shard_map/all_to_all | solution.py:153
  58.3 18.1 %all-to-all-start.5 = ((s32[128,1,8]{2,1,0:T(1,128)}), s32[128,1,8]{2,1,0:T(1,128)S(1)}, u32[]{:S(2)}, u32[]{:S(2)}) async-start(s32[128,1,8]{2,1,0:T(1,128)} %broadcast_in_dim.62), calls=%async_computation.5 | async-start | bytes 131072 | tf_op jit(solution)/shard_map/all_to_all | solution.py:153
  128.8 16.0 %all-to-all-start.4 = ((bf16[4,192,512]{2,1,0:T(8,128)(2,1)}), bf16[4,192,512]{2,1,0:T(8,128)(2,1)S(1)}, u32[]{:S(2)}, u32[]{:S(2)}) async-start(bf16[4,192,512]{2,1,0:T(8,128)(2,1)} %bitcast.9), calls=%async_computation.4 | async-start | bytes 1572864 | tf_op jit(solution)/shard_map/all_to_all | solution.py:153
  144.8 0.9 copy-start
  170.0 20.6 %all-to-all-start.7 = ((bf16[8,64,512]{2,1,0:T(8,128)(2,1)}), bf16[8,64,512]{2,1,0:T(8,128)(2,1)S(1)}, u32[]{:S(2)}, u32[]{:S(2)}) async-start(bf16[8,64,512]{2,1,0:T(8,128)(2,1)} %broadcast_in_dim.63), calls=%async_computation.7 | async-start | bytes 1048576 | tf_op jit(solution)/shard_map/all_to_all | solution.py:229
  190.6 0.8 copy-start.1
Sparse Core Ops, SparseCore 0:
  11.7 104.8 all-gather.1

commit v2 on v1

--- a/solution.py
+++ b/solution.py
@@ -7,7 +7,7 @@
 
 BF16 = jnp.bfloat16
 F32 = jnp.float32
-CAPACITY = 192
+CAPACITY = 176
 
 
 def matmul(a, b):
@@ -52,7 +52,7 @@
 
 
 def processor_kernel(
-    place, live, got, extra, edges, near, latent, w_first, w_second, n_first, n_second, edge_out, mesh_out, messages
+    place, live, got, extra, edges, near, latent, w_first, w_second, n_first, n_second, edge_out, mesh_out, copies, messages
 ):
     step, steps = pl.program_id(0), pl.num_programs(0)
     width = edges.shape[1]
@@ -70,10 +70,13 @@
     @pl.when(step == steps - 1)
     def _():
         node_pre = matmul(latent[...], n_first[:width]) + matmul(messages[...], n_first[width:])
-        mesh_out[...] = (latent[...].astype(F32) + second_layer(node_pre, n_second[...])).astype(BF16)
-
-
-def processor(place, live, got, extra, edges, latent, w_first, w_second, n_first, n_second, steps=4):
+        new = (latent[...].astype(F32) + second_layer(node_pre, n_second[...])).astype(BF16)
+        mesh_out[...] = new
+        for copy in range(copies.shape[0]):
+            copies[copy] = new
+
+
+def processor(place, live, got, extra, edges, latent, w_first, w_second, n_first, n_second, count, steps=2):
     slots, width = edges.shape
     nodes = latent.shape[0]
 
@@ -88,24 +91,20 @@
         grid=(steps,),
         in_specs=[tiles(place), tiles(live), whole(got), tiles(extra), tiles(edges), tiles(latent), whole(latent)]
         + [whole(w) for w in (w_first, w_second, n_first, n_second)],
-        out_specs=[tiles(edges), whole(latent)],
-        out_shape=[jax.ShapeDtypeStruct(edges.shape, BF16), jax.ShapeDtypeStruct(latent.shape, BF16)],
+        out_specs=[tiles(edges), whole(latent), pl.BlockSpec((count, *latent.shape), lambda i: (0, 0, 0))],
+        out_shape=[jax.ShapeDtypeStruct(a, BF16) for a in (edges.shape, latent.shape, (count, *latent.shape))],
         scratch_shapes=[pltpu.VMEM((nodes, width), BF16)],
         cost_estimate=pl.CostEstimate(flops=2_000_000_000, bytes_accessed=8_000_000, transcendentals=600_000),
         name="processor",
     )(place, live, got, extra, edges, latent, latent, w_first, w_second, n_first, n_second)
 
 
-def decoder_kernel(
-    named, index, near_a, near_b, edges, latent, w_first, w_second, n_first, n_second, head, out, sent
-):
+def decoder_first_kernel(named, index, near, edges, latent, w_first, out, sent):
     width = edges.shape[1]
 
     @pl.when(pl.program_id(0) == 0)
     def _():
-        columns = near_a.shape[0]
-        table = matmul(selection(named[...], columns), near_a[...])
-        table = table + matmul(selection(named[...] - columns, columns), near_b[...])
+        table = matmul(selection(named[...], near.shape[0]), near[...])
         sent[...] = matmul(table.astype(BF16), w_first[width : 2 * width]).astype(BF16)
 
     count, points = edges.shape[0], latent.shape[0]
@@ -113,49 +112,92 @@
     offset = lax.broadcasted_iota(jnp.int32, (count, points), 0) - fanin * lax.broadcasted_iota(
         jnp.int32, (count, points), 1
     )
+    receivers = matmul(marks((offset >= 0) & (offset < fanin)), latent[...]).astype(BF16)
+    pre = matmul(edges[...], w_first[:width]) + matmul(receivers, w_first[2 * width :])
+    out[...] = pre + matmul(selection(index[...], sent.shape[0]), sent[...])
+
+
+def tiles_of(array, steps):
+    return pl.BlockSpec((array.shape[0] // steps, array.shape[1]), lambda i: (i, 0))
+
+
+def whole_of(array):
+    return pl.BlockSpec(array.shape, lambda i: (0, 0))
+
+
+def decoder_first(named, index, near, edges, latent, w_first, steps=2):
+    out = jax.ShapeDtypeStruct(edges.shape, F32)
+    return pl.pallas_call(
+        decoder_first_kernel,
+        grid=(steps,),
+        in_specs=[
+            whole_of(named),
+            tiles_of(index, steps),
+            whole_of(near),
+            tiles_of(edges, steps),
+            tiles_of(latent, steps),
+            whole_of(w_first),
+        ],
+        out_specs=tiles_of(out, steps),
+        out_shape=out,
+        scratch_shapes=[pltpu.VMEM((named.shape[0], edges.shape[1]), BF16)],
+        cost_estimate=pl.CostEstimate(flops=2_000_000_000, bytes_accessed=6_000_000, transcendentals=0),
+        name="decoder_first",
+    )(named, index, near, edges, latent, w_first)
+
+
+def decoder_second_kernel(
+    start, index, far, first, edges, latent, w_send, w_second, n_first, n_second, head, out
+):
+    count, width = edges.shape
+    points = latent.shape[0]
+    fanin = count // points
     onto = lax.broadcasted_iota(jnp.int32, (points, count), 1) - fanin * lax.broadcasted_iota(
         jnp.int32, (points, count), 0
     )
-    receivers = matmul(marks((offset >= 0) & (offset < fanin)), latent[...]).astype(BF16)
-    pre = matmul(edges[...], w_first[:width]) + matmul(receivers, w_first[2 * width :])
-    pre = pre + matmul(selection(index[...], sent.shape[0]), sent[...])
+    sent = matmul(far[...], w_send[...]).astype(BF16)
+    pre = first[...] + matmul(selection(index[...] - start[0], sent.shape[0]), sent)
     updated = (edges[...].astype(F32) + second_layer(pre, w_second[...])).astype(BF16)
     summed = matmul(marks((onto >= 0) & (onto < fanin)), updated).astype(BF16)
     point_pre = matmul(latent[...], n_first[:width]) + matmul(summed, n_first[width:])
     point_new = (latent[...].astype(F32) + second_layer(point_pre, n_second[...])).astype(BF16)
-    out[...] = matmul(point_new, head[...])
-
-
-def decoder(named, index, near_a, near_b, edges, latent, w_first, w_second, n_first, n_second, head, steps=2):
-    width = edges.shape[1]
-
-    def tiles(array):
-        return pl.BlockSpec((array.shape[0] // steps, array.shape[1]), lambda i: (i, 0))
-
-    def whole(array):
-        return pl.BlockSpec(array.shape, lambda i: (0, 0))
-
-    out = jax.ShapeDtypeStruct((latent.shape[0], head.shape[1]), F32)
+    out[...] = lax.dot_general(
+        head[...], point_new, (((0,), (1,)), ((), ())), preferred_element_type=F32
+    )
+
+
+def decoder_second(start, index, far, first, edges, latent, w_first, w_second, n_first, n_second, head, steps=2):
+    points, width = latent.shape
+    channels = head.shape[1]
+    send = pl.BlockSpec((width, width), lambda i: (1, 0))
     return pl.pallas_call(
-        decoder_kernel,
+        decoder_second_kernel,
         grid=(steps,),
-        in_specs=[whole(named), tiles(index), whole(near_a), whole(near_b), tiles(edges), tiles(latent)]
-        + [whole(w) for w in (w_first, w_second, n_first, n_second, head)],
-        out_specs=tiles(out),
-        out_shape=out,
-        scratch_shapes=[pltpu.VMEM((named.shape[0], width), BF16)],
-        cost_estimate=pl.CostEstimate(flops=3_000_000_000, bytes_accessed=8_000_000, transcendentals=1_000_000),
-        name="decoder",
-    )(named, index, near_a, near_b, edges, latent, w_first, w_second, n_first, n_second, head)
+        in_specs=[
+            pl.BlockSpec(memory_space=pltpu.SMEM),
+            tiles_of(index, steps),
+            whole_of(far),
+            tiles_of(first, steps),
+            tiles_of(edges, steps),
+            tiles_of(latent, steps),
+            send,
+        ]
+        + [whole_of(w) for w in (w_second, n_first, n_second, head)],
+        out_specs=pl.BlockSpec((channels, points // steps), lambda i: (0, i)),
+        out_shape=jax.ShapeDtypeStruct((channels, points), F32),
+        cost_estimate=pl.CostEstimate(flops=2_000_000_000, bytes_accessed=6_000_000, transcendentals=1_000_000),
+        name="decoder_second",
+    )(start, index, far, first, edges, latent, w_first, w_second, n_first, n_second, head)
 
 
 def exchanged(blocks, axis):
     return lax.all_to_all(blocks, axis, split_axis=0, concat_axis=0, tiled=True)
 
 
-def passed_along(block, axis, distance):
+def swapped(block, axis, first):
     count = lax.axis_size(axis)
-    return lax.ppermute(block, axis, [((i - distance) % count, i) for i in range(count)])
+    pairs = [((first + i) % count, (first + (i ^ 1)) % count) for i in range(count)]
+    return lax.ppermute(block, axis, pairs)
 
 
 def one_hot(index, size):
@@ -219,17 +261,14 @@
     return jnp.max(exchanged(copies, "wide"))
 
 
-def two_patches(block, first):
-    group, peers = lax.axis_size("narrow"), lax.axis_size("wide")
-    count = group * peers
-    members = [
-        [(2 * group * k + first * group + j) % count for j in range(2 * group)] for k in range(peers // 2)
-    ]
-    copies = jnp.broadcast_to(block, (2 * group, *block.shape))
+def two_patches(copies):
+    group = copies.shape[0]
+    count = lax.axis_size("narrow") * lax.axis_size("wide")
+    members = [list(range(first, first + group)) for first in range(0, count, group)]
     got = lax.all_to_all(
         copies, ("wide", "narrow"), split_axis=0, concat_axis=0, axis_index_groups=members, tiled=True
     )
-    return got.reshape(-1, block.shape[1])
+    return got.reshape(-1, copies.shape[2])
 
 
 def body(
@@ -275,20 +314,24 @@
     lists = decoder_send_rows[0, 0]
     odd = lax.axis_index("wide") % 2
     span = nodes * group
+    after, before = lists[0], lists[1]
+    beside = swapped(jnp.where(odd == 1, before, after), "wide", 0) + (1 - odd) * span
+    outside = jnp.where(odd == 1, after, before) + odd * span
+    own = odd * span + jnp.arange(span, dtype=jnp.int32)
+    nowhere = jnp.full(beside.shape, -1, jnp.int32)
     named = jnp.concatenate(
-        [
-            odd * span + jnp.arange(span, dtype=jnp.int32),
-            (1 - odd) * 2 * span + passed_along(lists[0], "wide", 1),
-            (1 + 2 * odd) * span + passed_along(lists[1], "wide", -1),
-        ]
-    )
+        [own, jnp.where(odd == 1, beside, nowhere), jnp.where(odd == 1, nowhere, beside)]
+    )
+    start = (span + odd * beside.shape[0]).reshape(1)
     live = lax.broadcasted_iota(jnp.int32, (nodes, degree), 1) < mesh_degree[:, None]
-    place, live, named, index, ids = lax.optimization_barrier(
+    place, live, named, index, outside, start, ids = lax.optimization_barrier(
         (
             place.reshape(-1, 1),
             live.astype(F32).reshape(-1, 1),
             named.reshape(-1, 1),
             decoder_senders.reshape(-1, 1),
+            outside,
+            start,
             ids,
         )
     )
@@ -303,7 +346,7 @@
         return matmul(late, delivered(rows_of(table, late_ids))).astype(BF16)
 
     extra = lax.cond(most > CAPACITY, fetch_rest, lambda: jnp.zeros((slots, width), BF16))
-    edge_out, mesh_out = processor(
+    edge_out, mesh_out, copies = processor(
         place,
         live,
         got,
@@ -314,22 +357,27 @@
         weight(table, 12, 4),
         weight(table, 16, 8),
         weight(table, 24, 4),
+        2 * group,
     )
 
     late_table, _ = lax.optimization_barrier((table, mesh_out))
-    grid_pred = decoder(
-        named,
+    near = two_patches(copies)
+    far = swapped(matmul(one_hot(outside, near.shape[0]), near).astype(BF16), "wide", 1)
+    de_first = weight(late_table, 32, 12)
+    first = decoder_first(named, index, near, decoder_edges, grid_latent, de_first)
+    grid_pred = decoder_second(
+        start,
         index,
-        two_patches(mesh_out, 0),
-        two_patches(mesh_out, 1),
+        far,
+        first,
         decoder_edges,
         grid_latent,
-        weight(late_table, 32, 12),
+        de_first,
         weight(late_table, 44, 4),
         weight(late_table, 48, 8),
         weight(late_table, 56, 4),
         weight(late_table, 28, 4)[:, :channels],
-    )
+    ).T
     return (mesh_out, edge_out, grid_pred)
 
 

time: 210 us -> 194 us (0.924)
  blocking collectives: 14.1 us -> 0 us
  local copies, waits for them, and re-layouts: 45.7 us -> 41.3 us
  starting transfers between devices: 51.3 us -> 48 us
  waiting for transfers between devices: 57.9 us -> 60.6 us
  Pallas kernels: 19.1 us -> 21.3 us
    all_to_all x1 -> x0, blocking collectives: 14.1 us -> none  [two_patches(): lax.all_to_all(copies, ('wide', 'narrow'), split_axis=0, concat_axis=0, a...]
    pallas_call x1 -> x2, Pallas kernels: 9.01 us -> 12.5 us  [the longest x1 7.09 us: decoder_second(): pl.pallas_call(decoder_second_kernel, grid=(steps,), in_specs=[pl.BlockSp...]
    all_to_all x1, starting transfers between devices: 8.19 us -> 4.87 us  [two_patches(): lax.all_to_all(copies, ('wide', 'narrow'), split_axis=0, concat_axis=0, a...]
    ppermute x2, waiting for transfers between devices: 3.25 us -> 0.01 us  [swapped(): return lax.ppermute(block, axis, pairs)]
    all_gather x1, waiting for transfers between devices: 39.4 us -> 42.6 us  [body(): table = lax.all_gather(pack, 'wide', axis=0, tiled=True)]
    all_to_all x4, waiting for transfers between devices: 15.2 us -> 18 us  [exchanged(): return lax.all_to_all(blocks, axis, split_axis=0, concat_axis=0, tiled=True)]
    unnamed x9 -> x10, local copies, waits for them, and re-layouts: 6.48 us -> 4.53 us
  transfers between devices with their start and end apart: 8 -> 8, of which waited for: 5 -> 5; matrix products, arithmetic and copies ran while one was open for 16% -> 17% of each run, Pallas kernels for 0% -> 3%
where the time goes in v2:
time: 194 us; the launch traced here: 193 us
  waiting for transfers between devices  60.6 us (31%)
  starting transfers between devices  48 us (25%)
  local copies, waits for them, and re-layouts  41.3 us (21%)
  Pallas kernels  21.3 us (11%)
  between operations  15.6 us (8%)
  other arithmetic  4.85 us (2%)
    all_gather x1, waiting for transfers between devices, body(): table = lax.all_gather(pack, 'wide', axis=0, tiled=True)  42.6 us
    all_to_all x4, starting transfers between devices, exchanged(): return lax.all_to_all(blocks, axis, split_axis=0, concat_axis=0, tiled=True)  36 us
    all_to_all x4, waiting for transfers between devices, exchanged(): return lax.all_to_all(blocks, axis, split_axis=0, concat_axis=0, tiled=True)  18 us
    gather x1, local copies, waits for them, and re-layouts, rows_of(): return table.at[ids].get(mode='promise_in_bounds')  11.3 us
    reshape x9, local copies, waits for them, and re-layouts, weight(): return parts[:, nodes + first:nodes + first + count].reshape(-1, width)  11.1 us
    slice x4, local copies, waits for them, and re-layouts, weight(): return parts[:, nodes + first:nodes + first + count].reshape(-1, width)  8.06 us
    pallas_call x1, Pallas kernels, processor(): pl.pallas_call(processor_kernel, grid=(steps,), in_specs=[tiles(place), t...  7.25 us
    ppermute x2, starting transfers between devices, swapped(): return lax.ppermute(block, axis, pairs)  7.12 us
  transfers between devices with their start and end apart: 8, of which 5 were waited for; matrix products, arithmetic and copies ran while one was open for 17% of the time, Pallas kernels for 3%

profile of v2, /device:TPU:2, one launch (start us, length us, event | category | flops | bytes accessed | tf_op | source)
XLA Modules:
  0.0 193.2 jit_solution(17576139543594125573)
XLA Ops:
  7.2 1.6 pack.1
  8.8 1.4 copy.85
  10.3 17.8 %all-to-all-start.2 = ((s32[128,1,32]{2,1,0:T(1,128)}), s32[128,1,32]{2,1,0:T(1,128)S(1)}, u32[]{:S(2)}, u32[]{:S(2)}) async-start(s32[128,1,32]{2,1,0:T(1,128)} %bitcast.2), calls=%async_computation.2 | async-start | bytes 131072 | tf_op jit(solution)/shard_map/all_to_all | solution.py:194
  28.9 1.9 collective-permute-start
  33.9 5.3 %all-to-all-done.2 = s32[128,1,32]{2,1,0:T(1,128)S(1)} async-done(((s32[128,1,32]{2,1,0:T(1,128)}), s32[128,1,32]{2,1,0:T(1,128)S(1)}, u32[]{:S(2)}, u32[]{:S(2)}) %all-to-all-start.2) | async-done | bytes 16416 | tf_op jit(solution)/shard_map/all_to_all | solution.py:194
  42.8 4.8 %all-to-all-start.3 = ((s32[4,1,384]{2,1,0:T(1,128)}), s32[4,1,384]{2,1,0:T(1,128)S(1)}, u32[]{:S(2)}, u32[]{:S(2)}) async-start(s32[4,1,384]{2,1,0:T(1,128)} %all_to_all.37), calls=%async_computation.3 | async-start | bytes 12288 | tf_op jit(solution)/shard_map/all_to_all | solution.py:194
  47.6 0.9 fusion.29.place
  48.5 2.9 %all-to-all-done.3 = s32[4,1,384]{2,1,0:T(1,128)S(1)} async-done(((s32[4,1,384]{2,1,0:T(1,128)}), s32[4,1,384]{2,1,0:T(1,128)S(1)}, u32[]{:S(2)}, u32[]{:S(2)}) %all-to-all-start.3) | async-done | bytes 6176 | tf_op jit(solution)/shard_map/all_to_all | solution.py:194
  52.2 1.3 broadcast_in_dim.63
  53.5 8.6 %all-to-all-start.5 = ((s32[128,1,8]{2,1,0:T(1,128)}), s32[128,1,8]{2,1,0:T(1,128)S(1)}, u32[]{:S(2)}, u32[]{:S(2)}) async-start(s32[128,1,8]{2,1,0:T(1,128)} %broadcast_in_dim.63), calls=%async_computation.5 | async-start | bytes 131072 | tf_op jit(solution)/shard_map/all_to_all | solution.py:194
  63.0 0.9 copy.100.index
  64.8 8.4 %all-to-all-done.5 = s32[128,1,8]{2,1,0:T(1,128)S(1)} async-done(((s32[128,1,8]{2,1,0:T(1,128)}), s32[128,1,8]{2,1,0:T(1,128)S(1)}, u32[]{:S(2)}, u32[]{:S(2)}) %all-to-all-start.5) | async-done | bytes 4128 | tf_op jit(solution)/shard_map/all_to_all | solution.py:194
  74.0 42.6 %all-gather.2.cloned.1.call-done = bf16[16384,512]{1,0:T(8,128)(2,1)} async-done(((bf16[128,512]{1,0:T(8,128)(2,1)}), bf16[16384,512]{1,0:T(8,128)(2,1)}) %all-gather.2.cloned.1.call-update) | async-done | bytes 16777232 | tf_op jit(solution)/shard_map/all_gather | solution.py:302
  116.6 11.3 %gather_fusion.1 = bf16[704,512]{1,0:T(8,128)(2,1)} fusion(bf16[16384,512]{1,0:T(8,128)(2,1)} %all-gather.2.cloned.1.call-done, s32[1024]{0:T(1024)S(1)} %pad_clamp_fusion.1), kind=kCustom, calls=%fused_computation.1 | custom fusion | bytes 1444608 | tf_op jit(solution)/shard_map/gather | solution.py:251
  128.8 4.8 %all-to-all-start.4 = ((bf16[4,176,512]{2,1,0:T(8,128)(2,1)}), bf16[4,176,512]{2,1,0:T(8,128)(2,1)S(1)}, u32[]{:S(2)}, u32[]{:S(2)}) async-start(bf16[4,176,512]{2,1,0:T(8,128)(2,1)} %bitcast.10), calls=%async_computation.4 | async-start | bytes 1441792 | tf_op jit(solution)/shard_map/all_to_all | solution.py:194
  133.6 1.8 slice.86
  135.4 1.4 reshape.428.w_first
  136.8 2.0 %fusion.55 = (bf16[128,4,512]{2,1,0:T(4,128)(2,1)S(1)}, bf16[128,4,512]{2,1,0:T(4,128)(2,1)S(1)}) fusion(bf16[128,128,512]{2,1,0:T(8,128)(2,1)} %bitcast.33), kind=kLoop, calls=%fused_computation.124 | loop fusion | bytes 2097152 | tf_op jit(solution)/shard_map/slice | solution.py:306
  138.7 0.9 reshape.429.w_second
  140.6 2.2 %slice_bitcast_fusion.1.n_first = bf16[1024,512]{1,0:T(8,128)(2,1)} fusion(bf16[128,128,512]{2,1,0:T(8,128)(2,1)} %bitcast.34), kind=kLoop, calls=%fused_computation.47 | loop fusion | bytes 2097152 | tf_op jit(solution)/shard_map/reshape | solution.py:306
  142.8 1.3 all-to-all-done.4
  145.0 7.2 %processor.1 = (bf16[512,512]{1,0:T(8,128)(2,1)}, bf16[64,512]{1,0:T(8,128)(2,1)}, bf16[8,64,512]{2,1,0:T(8,128)(2,1)}) custom-call(s32[512,1]{1,0:T(8,128)} %fusion.29.place, f32[512,1]{1,0:T(8,128)} %copy.97.live, bf16[704,512]{1,0:T(8,128)(2,1)} %bitcast.42, bf16[512,512]{1,0:T(8,128)(2,1)S(1)} %get-tuple-element.138.extra, bf16[512,512]{1,0:T(8,128)(2,1)} %edges.3, ...), custom_call_target="tpu_custom_call" | custom-call | flops 2000000000 | bytes 8000000 | tf_op jit(solution)/shard_map/processor/pallas_call | solution.py:89
  152.3 4.9 %all-to-all-start.6 = ((bf16[8,64,512]{2,1,0:T(8,128)(2,1)}), bf16[8,64,512]{2,1,0:T(8,128)(2,1)S(1)}, u32[]{:S(2)}, u32[]{:S(2)}) async-start(bf16[8,64,512]{2,1,0:T(8,128)(2,1)} %get-tuple-element.110), calls=%async_computation.6 | async-start | bytes 1048576 | tf_op jit(solution)/shard_map/all_to_all | solution.py:268
  157.1 1.8 slice.90
  158.9 1.4 reshape.434.w_first.w_send
  160.3 2.5 %fusion.54 = (bf16[128,4,512]{2,1,0:T(4,128)(2,1)S(1)}, bf16[128,4,512]{2,1,0:T(4,128)(2,1)S(1)}, bf16[128,4,512]{2,1,0:T(4,128)(2,1)S(1)}) fusion(bf16[128,128,512]{2,1,0:T(8,128)(2,1)} %bitcast.36), kind=kLoop, calls=%fused_computation.123 | loop fusion | bytes 3145728 | tf_op jit(solution)/shard_map/slice | solution.py:306
  162.8 0.9 reshape.435.w_second
  163.8 0.9 reshape.437.n_second
  165.6 2.2 %slice_bitcast_fusion.n_first = bf16[1024,512]{1,0:T(8,128)(2,1)} fusion(bf16[128,128,512]{2,1,0:T(8,128)(2,1)} %bitcast.37), kind=kLoop, calls=%fused_computation.46 | loop fusion | bytes 2097152 | tf_op jit(solution)/shard_map/reshape | solution.py:306
  168.0 5.2 %collective-permute-start.1 = (bf16[32,512]{1,0:T(8,128)(2,1)S(1)}, bf16[32,512]{1,0:T(8,128)(2,1)S(1)}, u32[]{:S(2)}, u32[]{:S(2)}) collective-permute-start(bf16[32,512]{1,0:T(8,128)(2,1)S(1)} %convolution_convert_fusion), channel_id=1, source_target_pairs={{4,8},{8,4},{12,16},{16,12},{20,24},{24,20},{28,32},{32,28},{36,40... | collective-permute-start | bytes 98312 | tf_op jit(solution)/shard_map/ppermute | solution.py:200
  173.3 5.4 %decoder_first.1.first = f32[768,512]{1,0:T(8,128)} custom-call(s32[320,1]{1,0:T(8,128)} %copy.98.named, s32[768,1]{1,0:T(8,128)} %copy.100.index, bf16[512,512]{1,0:T(8,128)(2,1)} %bitcast.40, bf16[768,512]{1,0:T(8,128)(2,1)} %edges.5, bf16[256,512]{1,0:T(8,128)(2,1)} %latent.5, bf16[1536,512]{1,0:T(8,128)(2,1)} %reshape.434.w_first.w_send), custom_call_target="tpu_custom_call" | custom-call | flops 2000000000 | bytes 6000000 | tf_op jit(solution)/shard_map/decoder_first/pallas_call | solution.py:130
  179.2 7.1 %decoder_second.1 = f32[227,256]{1,0:T(8,128)} custom-call(s32[1]{0:T(128)} %bitcast.8.start, s32[768,1]{1,0:T(8,128)} %copy.100.index, bf16[32,512]{1,0:T(8,128)(2,1)} %copy-done.2, f32[768,512]{1,0:T(8,128)} %decoder_first.1.first, bf16[768,512]{1,0:T(8,128)(2,1)} %edges.5, bf16[256,512]{1,0:T(8,128)(2,1)} %latent.5, ...), custom_call_target="tpu_custom_call" | custom-call | flops 2000000000 | bytes 6000000 | tf_op jit(solution)/shard_map/decoder_second/pallas_call | solution.py:173
  (63 shorter events, 13.8 us)
Async XLA Ops:
  7.2 109.4 %all-gather.2.cloned.1.call-start = ((), (), s32[]{:S(2)}) async-start(), calls=%async_computation.7 | async-start | bytes 16908288 | tf_op jit(solution)/shard_map/all_gather | solution.py:302
  10.3 28.9 %all-to-all-start.2 = ((s32[128,1,32]{2,1,0:T(1,128)}), s32[128,1,32]{2,1,0:T(1,128)S(1)}, u32[]{:S(2)}, u32[]{:S(2)}) async-start(s32[128,1,32]{2,1,0:T(1,128)} %bitcast.2), calls=%async_computation.2 | async-start | bytes 131072 | tf_op jit(solution)/shard_map/all_to_all | solution.py:194
  28.9 4.9 %collective-permute-start = (s32[32]{0:T(128)S(1)}, s32[32]{0:T(128)S(1)}, u32[]{:S(2)}, u32[]{:S(2)}) collective-permute-start(s32[32]{0:T(128)S(1)} %get-tuple-element.133), channel_id=1, source_target_pairs={{0,4},{4,0},{8,12},{12,8},{16,20},{20,16},{24,28},{28,24},{32,36},... | collective-permute-start | bytes 392 | tf_op jit(solution)/shard_map/ppermute | solution.py:200
  42.8 8.7 %all-to-all-start.3 = ((s32[4,1,384]{2,1,0:T(1,128)}), s32[4,1,384]{2,1,0:T(1,128)S(1)}, u32[]{:S(2)}, u32[]{:S(2)}) async-start(s32[4,1,384]{2,1,0:T(1,128)} %all_to_all.37), calls=%async_computation.3 | async-start | bytes 12288 | tf_op jit(solution)/shard_map/all_to_all | solution.py:194
  53.5 19.7 %all-to-all-start.5 = ((s32[128,1,8]{2,1,0:T(1,128)}), s32[128,1,8]{2,1,0:T(1,128)S(1)}, u32[]{:S(2)}, u32[]{:S(2)}) async-start(s32[128,1,8]{2,1,0:T(1,128)} %broadcast_in_dim.63), calls=%async_computation.5 | async-start | bytes 131072 | tf_op jit(solution)/shard_map/all_to_all | solution.py:194
  128.8 15.4 %all-to-all-start.4 = ((bf16[4,176,512]{2,1,0:T(8,128)(2,1)}), bf16[4,176,512]{2,1,0:T(8,128)(2,1)S(1)}, u32[]{:S(2)}, u32[]{:S(2)}) async-start(bf16[4,176,512]{2,1,0:T(8,128)(2,1)} %bitcast.10), calls=%async_computation.4 | async-start | bytes 1441792 | tf_op jit(solution)/shard_map/all_to_all | solution.py:194
  144.2 0.9 copy-start.1
  152.3 15.5 %all-to-all-start.6 = ((bf16[8,64,512]{2,1,0:T(8,128)(2,1)}), bf16[8,64,512]{2,1,0:T(8,128)(2,1)S(1)}, u32[]{:S(2)}, u32[]{:S(2)}) async-start(bf16[8,64,512]{2,1,0:T(8,128)(2,1)} %get-tuple-element.110), calls=%async_computation.6 | async-start | bytes 1048576 | tf_op jit(solution)/shard_map/all_to_all | solution.py:268
  167.8 5.4 %copy-start = (bf16[8,64,512]{2,1,0:T(8,128)(2,1)}, bf16[8,64,512]{2,1,0:T(8,128)(2,1)S(1)}, u32[]{:S(2)}) copy-start(bf16[8,64,512]{2,1,0:T(8,128)(2,1)S(1)} %all-to-all-done.6) | copy-start | bytes 1572868
  168.0 10.6 %collective-permute-start.1 = (bf16[32,512]{1,0:T(8,128)(2,1)S(1)}, bf16[32,512]{1,0:T(8,128)(2,1)S(1)}, u32[]{:S(2)}, u32[]{:S(2)}) collective-permute-start(bf16[32,512]{1,0:T(8,128)(2,1)S(1)} %convolution_convert_fusion), channel_id=1, source_target_pairs={{4,8},{8,4},{12,16},{16,12},{20,24},{24,20},{28,32},{32,28},{36,40... | collective-permute-start | bytes 98312 | tf_op jit(solution)/shard_map/ppermute | solution.py:200
  178.6 0.6 copy-start.2
Sparse Core Ops, SparseCore 0:
  11.7 104.8 all-gather.1

commit v3 on v2

--- a/solution.py
+++ b/solution.py
@@ -49,6 +49,55 @@
         scratch_shapes=[pltpu.VMEM((rows, width), F32)],
         name="pack",
     )(*pieces)
+
+
+def rows_in(gathered, first, rows):
+    shards, _, width = gathered.shape
+    count = rows // shards
+    return pl.BlockSpec((shards, count, width), lambda *_: (0, first // count, 0))
+
+
+def gather_kernel(ids, place, table, out, stage, sems):
+    halves = sems.shape[0]
+    count, block, width = stage.shape
+    share = count // halves
+
+    for half in range(halves):
+
+        def begin(i, carry, half=half):
+            row = half * share + i
+            pltpu.make_async_copy(table.at[ids[row]], stage.at[row], sems.at[half]).start()
+            return carry
+
+        lax.fori_loop(0, share, begin, 0, unroll=8)
+
+    batch = 256 // block
+    column = lax.broadcasted_iota(jnp.int32, (batch, batch * block), 1)
+    first = block * lax.broadcasted_iota(jnp.int32, (batch, batch * block), 0)
+    for half in range(halves):
+        mine = pl.ds(half * share, share)
+        pltpu.make_async_copy(table.at[pl.ds(0, share)], stage.at[mine], sems.at[half]).wait()
+        for k in range(share // batch):
+            rows = pl.ds(half * share + k * batch, batch)
+            pick = marks(column == first + place[rows])
+            out[rows] = matmul(pick, stage[rows].reshape(batch * block, width)).astype(BF16)
+
+
+def rows_of_blocks(table, ids, block=8, halves=2):
+    count, width = ids.shape[0], table.shape[1]
+    return pl.pallas_call(
+        gather_kernel,
+        in_specs=[
+            pl.BlockSpec(memory_space=pltpu.SMEM),
+            pl.BlockSpec(memory_space=pltpu.VMEM),
+            pl.BlockSpec(memory_space=pl.ANY),
+        ],
+        out_specs=pl.BlockSpec(memory_space=pltpu.VMEM),
+        out_shape=jax.ShapeDtypeStruct((count, width), BF16),
+        scratch_shapes=[pltpu.VMEM((count, block, width), BF16), pltpu.SemaphoreType.DMA((halves,))],
+        cost_estimate=pl.CostEstimate(flops=1_000_000_000, bytes_accessed=6_000_000, transcendentals=0),
+        name="rows",
+    )(ids // block, (ids % block).reshape(-1, 1), table.reshape(-1, block, width))
 
 
 def processor_kernel(
@@ -69,14 +118,15 @@
 
     @pl.when(step == steps - 1)
     def _():
-        node_pre = matmul(latent[...], n_first[:width]) + matmul(messages[...], n_first[width:])
+        inner = n_first[...].reshape(2 * width, width)
+        node_pre = matmul(latent[...], inner[:width]) + matmul(messages[...], inner[width:])
         new = (latent[...].astype(F32) + second_layer(node_pre, n_second[...])).astype(BF16)
         mesh_out[...] = new
         for copy in range(copies.shape[0]):
             copies[copy] = new
 
 
-def processor(place, live, got, extra, edges, latent, w_first, w_second, n_first, n_second, count, steps=2):
+def processor(place, live, got, extra, edges, latent, w_first, w_second, n_first, n_at, n_second, count, steps=2):
     slots, width = edges.shape
     nodes = latent.shape[0]
 
@@ -90,7 +140,7 @@
         processor_kernel,
         grid=(steps,),
         in_specs=[tiles(place), tiles(live), whole(got), tiles(extra), tiles(edges), tiles(latent), whole(latent)]
-        + [whole(w) for w in (w_first, w_second, n_first, n_second)],
+        + [whole(w_first), whole(w_second), rows_in(n_first, n_at, 2 * width), whole(n_second)],
         out_specs=[tiles(edges), whole(latent), pl.BlockSpec((count, *latent.shape), lambda i: (0, 0, 0))],
         out_shape=[jax.ShapeDtypeStruct(a, BF16) for a in (edges.shape, latent.shape, (count, *latent.shape))],
         scratch_shapes=[pltpu.VMEM((nodes, width), BF16)],
@@ -159,14 +209,15 @@
     pre = first[...] + matmul(selection(index[...] - start[0], sent.shape[0]), sent)
     updated = (edges[...].astype(F32) + second_layer(pre, w_second[...])).astype(BF16)
     summed = matmul(marks((onto >= 0) & (onto < fanin)), updated).astype(BF16)
-    point_pre = matmul(latent[...], n_first[:width]) + matmul(summed, n_first[width:])
+    inner = n_first[...].reshape(2 * width, width)
+    point_pre = matmul(latent[...], inner[:width]) + matmul(summed, inner[width:])
     point_new = (latent[...].astype(F32) + second_layer(point_pre, n_second[...])).astype(BF16)
     out[...] = lax.dot_general(
         head[...], point_new, (((0,), (1,)), ((), ())), preferred_element_type=F32
     )
 
 
-def decoder_second(start, index, far, first, edges, latent, w_first, w_second, n_first, n_second, head, steps=2):
+def decoder_second(start, index, far, first, edges, latent, w_first, w_second, n_first, n_at, n_second, head, steps=2):
     points, width = latent.shape
     channels = head.shape[1]
     send = pl.BlockSpec((width, width), lambda i: (1, 0))
@@ -182,7 +233,7 @@
             tiles_of(latent, steps),
             send,
         ]
-        + [whole_of(w) for w in (w_second, n_first, n_second, head)],
+        + [whole_of(w_second), rows_in(n_first, n_at, 2 * width), whole_of(n_second), whole_of(head)],
         out_specs=pl.BlockSpec((channels, points // steps), lambda i: (0, i)),
         out_shape=jax.ShapeDtypeStruct((channels, points), F32),
         cost_estimate=pl.CostEstimate(flops=2_000_000_000, bytes_accessed=6_000_000, transcendentals=1_000_000),
@@ -335,7 +386,7 @@
             ids,
         )
     )
-    found = rows_of(table, ids)
+    found = rows_of_blocks(table, ids)
     got = delivered(found)
     most, _ = lax.optimization_barrier((most, found))
 
@@ -355,7 +406,8 @@
         mesh_latent,
         weight(table, 0, 12),
         weight(table, 12, 4),
-        weight(table, 16, 8),
+        table.reshape(-1, stride, width),
+        nodes + 16,
         weight(table, 24, 4),
         2 * group,
     )
@@ -374,7 +426,8 @@
         grid_latent,
         de_first,
         weight(late_table, 44, 4),
-        weight(late_table, 48, 8),
+        late_table.reshape(-1, stride, width),
+        nodes + 48,
         weight(late_table, 56, 4),
         weight(late_table, 28, 4)[:, :channels],
     ).T

time: 194 us -> 194 us (level)
  local copies, waits for them, and re-layouts: 41.3 us -> 26.4 us
  Pallas kernels: 21.3 us -> 33.9 us
  waiting for transfers between devices: 60.6 us -> 63.6 us
    pallas_call x0 -> x1, Pallas kernels: none -> 12.6 us  [rows_of_blocks(): pl.pallas_call(gather_kernel, in_specs=[pl.BlockSpec(memory_space=pltpu.S...]
    gather x1 -> x0, local copies, waits for them, and re-layouts: 11.3 us -> none  [rows_of(): return table.at[ids].get(mode='promise_in_bounds')]
    reshape x9 -> x7, local copies, waits for them, and re-layouts: 11.1 us -> 6.51 us  [weight(): return parts[:, nodes + first:nodes + first + count].reshape(-1, width)]
    all_to_all x4, waiting for transfers between devices: 18 us -> 21.1 us  [exchanged(): return lax.all_to_all(blocks, axis, split_axis=0, concat_axis=0, tiled=True)]
  transfers between devices with their start and end apart: 8 -> 8, of which waited for: 5 -> 5; matrix products, arithmetic and copies ran while one was open for 17% -> 16% of each run, Pallas kernels for 3% -> 3%
where the time goes in v3:
time: 194 us; the launch traced here: 193 us
  waiting for transfers between devices  63.6 us (33%)
  starting transfers between devices  46.6 us (24%)
  Pallas kernels  33.9 us (17%)
  local copies, waits for them, and re-layouts  26.4 us (14%)
  between operations  15.6 us (8%)
  other arithmetic  5.41 us (3%)
    all_gather x1, waiting for transfers between devices, body(): table = lax.all_gather(pack, 'wide', axis=0, tiled=True)  42.5 us
    all_to_all x4, starting transfers between devices, exchanged(): return lax.all_to_all(blocks, axis, split_axis=0, concat_axis=0, tiled=True)  34.7 us
    all_to_all x4, waiting for transfers between devices, exchanged(): return lax.all_to_all(blocks, axis, split_axis=0, concat_axis=0, tiled=True)  21.1 us
    pallas_call x1, Pallas kernels, rows_of_blocks(): pl.pallas_call(gather_kernel, in_specs=[pl.BlockSpec(memory_space=pltpu.S...  12.6 us
    slice x4, local copies, waits for them, and re-layouts, weight(): return parts[:, nodes + first:nodes + first + count].reshape(-1, width)  8.06 us
    pallas_call x1, Pallas kernels, processor(): pl.pallas_call(processor_kernel, grid=(steps,), in_specs=[tiles(place), t...  7.28 us
    pallas_call x1, Pallas kernels, decoder_second(): pl.pallas_call(decoder_second_kernel, grid=(steps,), in_specs=[pl.BlockSp...  7.09 us
    ppermute x2, starting transfers between devices, swapped(): return lax.ppermute(block, axis, pairs)  7.06 us
  transfers between devices with their start and end apart: 8, of which 5 were waited for; matrix products, arithmetic and copies ran while one was open for 16% of the time, Pallas kernels for 3%

profile of v3, /device:TPU:2, one launch (start us, length us, event | category | flops | bytes accessed | tf_op | source)
XLA Modules:
  0.0 193.1 jit_solution(7787286098496830443)
XLA Ops:
  7.2 1.6 pack.1
  8.8 1.4 copy.89
  10.3 17.8 %all-to-all-start.2 = ((s32[128,1,32]{2,1,0:T(1,128)}), s32[128,1,32]{2,1,0:T(1,128)S(1)}, u32[]{:S(2)}, u32[]{:S(2)}) async-start(s32[128,1,32]{2,1,0:T(1,128)} %bitcast.2), calls=%async_computation.2 | async-start | bytes 131072 | tf_op jit(solution)/shard_map/all_to_all | solution.py:245
  28.9 1.9 collective-permute-start
  33.9 5.3 %all-to-all-done.2 = s32[128,1,32]{2,1,0:T(1,128)S(1)} async-done(((s32[128,1,32]{2,1,0:T(1,128)}), s32[128,1,32]{2,1,0:T(1,128)S(1)}, u32[]{:S(2)}, u32[]{:S(2)}) %all-to-all-start.2) | async-done | bytes 16416 | tf_op jit(solution)/shard_map/all_to_all | solution.py:245
  42.8 4.8 %all-to-all-start.3 = ((s32[4,1,384]{2,1,0:T(1,128)}), s32[4,1,384]{2,1,0:T(1,128)S(1)}, u32[]{:S(2)}, u32[]{:S(2)}) async-start(s32[4,1,384]{2,1,0:T(1,128)} %all_to_all.37), calls=%async_computation.3 | async-start | bytes 12288 | tf_op jit(solution)/shard_map/all_to_all | solution.py:245
  47.6 0.9 fusion.29.place
  48.5 2.9 %all-to-all-done.3 = s32[4,1,384]{2,1,0:T(1,128)S(1)} async-done(((s32[4,1,384]{2,1,0:T(1,128)}), s32[4,1,384]{2,1,0:T(1,128)S(1)}, u32[]{:S(2)}, u32[]{:S(2)}) %all-to-all-start.3) | async-done | bytes 6176 | tf_op jit(solution)/shard_map/all_to_all | solution.py:245
  52.2 1.3 broadcast_in_dim.59
  53.5 8.6 %all-to-all-start.5 = ((s32[128,1,8]{2,1,0:T(1,128)}), s32[128,1,8]{2,1,0:T(1,128)S(1)}, u32[]{:S(2)}, u32[]{:S(2)}) async-start(s32[128,1,8]{2,1,0:T(1,128)} %broadcast_in_dim.59), calls=%async_computation.5 | async-start | bytes 131072 | tf_op jit(solution)/shard_map/all_to_all | solution.py:245
  62.7 0.9 reshape.448.place
  63.6 9.6 %all-to-all-done.5 = s32[128,1,8]{2,1,0:T(1,128)S(1)} async-done(((s32[128,1,8]{2,1,0:T(1,128)}), s32[128,1,8]{2,1,0:T(1,128)S(1)}, u32[]{:S(2)}, u32[]{:S(2)}) %all-to-all-start.5) | async-done | bytes 4128 | tf_op jit(solution)/shard_map/all_to_all | solution.py:245
  74.0 42.5 %all-gather.2.cloned.1.call-done = bf16[16384,512]{1,0:T(8,128)(2,1)} async-done(((bf16[128,512]{1,0:T(8,128)(2,1)}), bf16[16384,512]{1,0:T(8,128)(2,1)}) %all-gather.2.cloned.1.call-update) | async-done | bytes 16777232 | tf_op jit(solution)/shard_map/all_gather | solution.py:353
  116.5 12.6 %rows.1 = bf16[704,512]{1,0:T(8,128)(2,1)} custom-call(s32[704]{0:T(1024)} %get-tuple-element.124.ids, s32[704,1]{1,0:T(8,128)} %reshape.448.place, bf16[2048,8,512]{2,1,0:T(8,128)(2,1)} %bitcast.29), custom_call_target="tpu_custom_call" | custom-call | flops 1000000000 | bytes 6000000 | tf_op jit(solution)/shard_map/rows/pallas_call | solution.py:88
  130.1 3.5 %all-to-all-start.4 = ((bf16[4,176,512]{2,1,0:T(8,128)(2,1)}), bf16[4,176,512]{2,1,0:T(8,128)(2,1)S(1)}, u32[]{:S(2)}, u32[]{:S(2)}) async-start(bf16[4,176,512]{2,1,0:T(8,128)(2,1)} %bitcast.11), calls=%async_computation.4 | async-start | bytes 1441792 | tf_op jit(solution)/shard_map/all_to_all | solution.py:245
  134.4 1.8 slice.76
  136.2 1.4 reshape.430.w_first
  137.5 2.0 %fusion.57 = (bf16[128,4,512]{2,1,0:T(4,128)(2,1)S(1)}, bf16[128,4,512]{2,1,0:T(4,128)(2,1)S(1)}) fusion(bf16[128,128,512]{2,1,0:T(8,128)(2,1)} %bitcast.31), kind=kLoop, calls=%fused_computation.127 | loop fusion | bytes 2097152 | tf_op jit(solution)/shard_map/slice | solution.py:357
  139.5 0.9 reshape.431.w_second
  140.4 0.9 reshape.432.n_second
  141.4 3.3 %all-to-all-done.4 = bf16[4,176,512]{2,1,0:T(8,128)(2,1)S(1)} async-done(((bf16[4,176,512]{2,1,0:T(8,128)(2,1)}), bf16[4,176,512]{2,1,0:T(8,128)(2,1)S(1)}, u32[]{:S(2)}, u32[]{:S(2)}) %all-to-all-start.4) | async-done | bytes 720928 | tf_op jit(solution)/shard_map/all_to_all | solution.py:245
  145.5 7.3 %processor.1 = (bf16[512,512]{1,0:T(8,128)(2,1)}, bf16[64,512]{1,0:T(8,128)(2,1)}, bf16[8,64,512]{2,1,0:T(8,128)(2,1)}) custom-call(s32[512,1]{1,0:T(8,128)} %fusion.29.place, f32[512,1]{1,0:T(8,128)} %copy.102.live, bf16[704,512]{1,0:T(8,128)(2,1)} %bitcast.37, bf16[512,512]{1,0:T(8,128)(2,1)S(1)} %get-tuple-element.140.extra, bf16[512,512]{1,0:T(8,128)(2,1)} %edges.3, ...), custom_call_target="tpu_custom_call" | custom-call | flops 2000000000 | bytes 8000000 | tf_op jit(solution)/shard_map/processor/pallas_call | solution.py:139
  152.8 4.9 %all-to-all-start.6 = ((bf16[8,64,512]{2,1,0:T(8,128)(2,1)}), bf16[8,64,512]{2,1,0:T(8,128)(2,1)S(1)}, u32[]{:S(2)}, u32[]{:S(2)}) async-start(bf16[8,64,512]{2,1,0:T(8,128)(2,1)} %get-tuple-element.110), calls=%async_computation.6 | async-start | bytes 1048576 | tf_op jit(solution)/shard_map/all_to_all | solution.py:319
  157.6 1.0 copy.105.index
  159.4 1.8 slice.79
  161.2 1.4 reshape.435.w_first.w_send
  162.6 2.5 %fusion.56 = (bf16[128,4,512]{2,1,0:T(4,128)(2,1)S(1)}, bf16[128,4,512]{2,1,0:T(4,128)(2,1)S(1)}, bf16[128,4,512]{2,1,0:T(4,128)(2,1)S(1)}) fusion(bf16[128,128,512]{2,1,0:T(8,128)(2,1)} %bitcast.34), kind=kLoop, calls=%fused_computation.126 | loop fusion | bytes 3145728 | tf_op jit(solution)/shard_map/slice | solution.py:357
  165.1 0.9 reshape.436.w_second
  166.0 0.9 reshape.437.n_second
  168.0 5.2 %collective-permute-start.1 = (bf16[32,512]{1,0:T(8,128)(2,1)S(1)}, bf16[32,512]{1,0:T(8,128)(2,1)S(1)}, u32[]{:S(2)}, u32[]{:S(2)}) collective-permute-start(bf16[32,512]{1,0:T(8,128)(2,1)S(1)} %convolution_convert_fusion), channel_id=1, source_target_pairs={{4,8},{8,4},{12,16},{16,12},{20,24},{24,20},{28,32},{32,28},{36,40... | collective-permute-start | bytes 98312 | tf_op jit(solution)/shard_map/ppermute | solution.py:251
  173.2 5.3 %decoder_first.1.first = f32[768,512]{1,0:T(8,128)} custom-call(s32[320,1]{1,0:T(8,128)} %copy.103.named, s32[768,1]{1,0:T(8,128)} %copy.105.index, bf16[512,512]{1,0:T(8,128)(2,1)} %bitcast.39, bf16[768,512]{1,0:T(8,128)(2,1)} %edges.5, bf16[256,512]{1,0:T(8,128)(2,1)} %latent.5, bf16[1536,512]{1,0:T(8,128)(2,1)} %reshape.435.w_first.w_send), custom_call_target="tpu_custom_call" | custom-call | flops 2000000000 | bytes 6000000 | tf_op jit(solution)/shard_map/decoder_first/pallas_call | solution.py:180
  179.1 7.1 %decoder_second.1 = f32[227,256]{1,0:T(8,128)} custom-call(s32[1]{0:T(128)} %bitcast.8.start, s32[768,1]{1,0:T(8,128)} %copy.105.index, bf16[32,512]{1,0:T(8,128)(2,1)} %copy-done.2, f32[768,512]{1,0:T(8,128)} %decoder_first.1.first, bf16[768,512]{1,0:T(8,128)(2,1)} %edges.5, bf16[256,512]{1,0:T(8,128)(2,1)} %latent.5, ...), custom_call_target="tpu_custom_call" | custom-call | flops 2000000000 | bytes 6000000 | tf_op jit(solution)/shard_map/decoder_second/pallas_call | solution.py:224
  (61 shorter events, 13.4 us)
Async XLA Ops:
  7.2 109.3 %all-gather.2.cloned.1.call-start = ((), (), s32[]{:S(2)}) async-start(), calls=%async_computation.7 | async-start | bytes 16908288 | tf_op jit(solution)/shard_map/all_gather | solution.py:353
  10.3 28.9 %all-to-all-start.2 = ((s32[128,1,32]{2,1,0:T(1,128)}), s32[128,1,32]{2,1,0:T(1,128)S(1)}, u32[]{:S(2)}, u32[]{:S(2)}) async-start(s32[128,1,32]{2,1,0:T(1,128)} %bitcast.2), calls=%async_computation.2 | async-start | bytes 131072 | tf_op jit(solution)/shard_map/all_to_all | solution.py:245
  28.9 4.9 %collective-permute-start = (s32[32]{0:T(128)S(1)}, s32[32]{0:T(128)S(1)}, u32[]{:S(2)}, u32[]{:S(2)}) collective-permute-start(s32[32]{0:T(128)S(1)} %get-tuple-element.135), channel_id=1, source_target_pairs={{0,4},{4,0},{8,12},{12,8},{16,20},{20,16},{24,28},{28,24},{32,36},... | collective-permute-start | bytes 392 | tf_op jit(solution)/shard_map/ppermute | solution.py:251
  42.8 8.7 %all-to-all-start.3 = ((s32[4,1,384]{2,1,0:T(1,128)}), s32[4,1,384]{2,1,0:T(1,128)S(1)}, u32[]{:S(2)}, u32[]{:S(2)}) async-start(s32[4,1,384]{2,1,0:T(1,128)} %all_to_all.37), calls=%async_computation.3 | async-start | bytes 12288 | tf_op jit(solution)/shard_map/all_to_all | solution.py:245
  53.5 19.7 %all-to-all-start.5 = ((s32[128,1,8]{2,1,0:T(1,128)}), s32[128,1,8]{2,1,0:T(1,128)S(1)}, u32[]{:S(2)}, u32[]{:S(2)}) async-start(s32[128,1,8]{2,1,0:T(1,128)} %broadcast_in_dim.59), calls=%async_computation.5 | async-start | bytes 131072 | tf_op jit(solution)/shard_map/all_to_all | solution.py:245
  130.1 14.6 %all-to-all-start.4 = ((bf16[4,176,512]{2,1,0:T(8,128)(2,1)}), bf16[4,176,512]{2,1,0:T(8,128)(2,1)S(1)}, u32[]{:S(2)}, u32[]{:S(2)}) async-start(bf16[4,176,512]{2,1,0:T(8,128)(2,1)} %bitcast.11), calls=%async_computation.4 | async-start | bytes 1441792 | tf_op jit(solution)/shard_map/all_to_all | solution.py:245
  144.6 0.9 copy-start
  152.8 15.0 %all-to-all-start.6 = ((bf16[8,64,512]{2,1,0:T(8,128)(2,1)}), bf16[8,64,512]{2,1,0:T(8,128)(2,1)S(1)}, u32[]{:S(2)}, u32[]{:S(2)}) async-start(bf16[8,64,512]{2,1,0:T(8,128)(2,1)} %get-tuple-element.110), calls=%async_computation.6 | async-start | bytes 1048576 | tf_op jit(solution)/shard_map/all_to_all | solution.py:319
  167.8 5.4 %copy-start.1 = (bf16[8,64,512]{2,1,0:T(8,128)(2,1)}, bf16[8,64,512]{2,1,0:T(8,128)(2,1)S(1)}, u32[]{:S(2)}) copy-start(bf16[8,64,512]{2,1,0:T(8,128)(2,1)S(1)} %all-to-all-done.6) | copy-start | bytes 1572868
  168.0 10.5 %collective-permute-start.1 = (bf16[32,512]{1,0:T(8,128)(2,1)S(1)}, bf16[32,512]{1,0:T(8,128)(2,1)S(1)}, u32[]{:S(2)}, u32[]{:S(2)}) collective-permute-start(bf16[32,512]{1,0:T(8,128)(2,1)S(1)} %convolution_convert_fusion), channel_id=1, source_target_pairs={{4,8},{8,4},{12,16},{16,12},{20,24},{24,20},{28,32},{32,28},{36,40... | collective-permute-start | bytes 98312 | tf_op jit(solution)/shard_map/ppermute | solution.py:251
  178.5 0.6 copy-start.2
Sparse Core Ops, SparseCore 0:
  11.7 104.7 all-gather.1

commit v4 on v2

--- a/solution.py
+++ b/solution.py
@@ -49,6 +49,26 @@
         scratch_shapes=[pltpu.VMEM((rows, width), F32)],
         name="pack",
     )(*pieces)
+
+
+def rows_in(gathered, first, rows):
+    shards, _, width = gathered.shape
+    count = rows // shards
+    return pl.BlockSpec((shards, count, width), lambda *_: (0, first // count, 0))
+
+
+def keep_kernel(*refs):
+    half = len(refs) // 2
+    for source, target in zip(refs[:half], refs[half:]):
+        target[...] = source[...]
+
+
+def kept(columns):
+    return pl.pallas_call(
+        keep_kernel,
+        out_shape=[jax.ShapeDtypeStruct(c.shape, c.dtype) for c in columns],
+        name="columns",
+    )(*columns)
 
 
 def processor_kernel(
@@ -69,14 +89,15 @@
 
     @pl.when(step == steps - 1)
     def _():
-        node_pre = matmul(latent[...], n_first[:width]) + matmul(messages[...], n_first[width:])
+        inner = n_first[...].reshape(2 * width, width)
+        node_pre = matmul(latent[...], inner[:width]) + matmul(messages[...], inner[width:])
         new = (latent[...].astype(F32) + second_layer(node_pre, n_second[...])).astype(BF16)
         mesh_out[...] = new
         for copy in range(copies.shape[0]):
             copies[copy] = new
 
 
-def processor(place, live, got, extra, edges, latent, w_first, w_second, n_first, n_second, count, steps=2):
+def processor(place, live, got, extra, edges, latent, w_first, w_second, n_first, n_at, n_second, count, steps=2):
     slots, width = edges.shape
     nodes = latent.shape[0]
 
@@ -90,7 +111,7 @@
         processor_kernel,
         grid=(steps,),
         in_specs=[tiles(place), tiles(live), whole(got), tiles(extra), tiles(edges), tiles(latent), whole(latent)]
-        + [whole(w) for w in (w_first, w_second, n_first, n_second)],
+        + [whole(w_first), whole(w_second), rows_in(n_first, n_at, 2 * width), whole(n_second)],
         out_specs=[tiles(edges), whole(latent), pl.BlockSpec((count, *latent.shape), lambda i: (0, 0, 0))],
         out_shape=[jax.ShapeDtypeStruct(a, BF16) for a in (edges.shape, latent.shape, (count, *latent.shape))],
         scratch_shapes=[pltpu.VMEM((nodes, width), BF16)],
@@ -159,14 +180,15 @@
     pre = first[...] + matmul(selection(index[...] - start[0], sent.shape[0]), sent)
     updated = (edges[...].astype(F32) + second_layer(pre, w_second[...])).astype(BF16)
     summed = matmul(marks((onto >= 0) & (onto < fanin)), updated).astype(BF16)
-    point_pre = matmul(latent[...], n_first[:width]) + matmul(summed, n_first[width:])
+    inner = n_first[...].reshape(2 * width, width)
+    point_pre = matmul(latent[...], inner[:width]) + matmul(summed, inner[width:])
     point_new = (latent[...].astype(F32) + second_layer(point_pre, n_second[...])).astype(BF16)
     out[...] = lax.dot_general(
         head[...], point_new, (((0,), (1,)), ((), ())), preferred_element_type=F32
     )
 
 
-def decoder_second(start, index, far, first, edges, latent, w_first, w_second, n_first, n_second, head, steps=2):
+def decoder_second(start, index, far, first, edges, latent, w_first, w_second, n_first, n_at, n_second, head, steps=2):
     points, width = latent.shape
     channels = head.shape[1]
     send = pl.BlockSpec((width, width), lambda i: (1, 0))
@@ -182,7 +204,7 @@
             tiles_of(latent, steps),
             send,
         ]
-        + [whole_of(w) for w in (w_second, n_first, n_second, head)],
+        + [whole_of(w_second), rows_in(n_first, n_at, 2 * width), whole_of(n_second), whole_of(head)],
         out_specs=pl.BlockSpec((channels, points // steps), lambda i: (0, i)),
         out_shape=jax.ShapeDtypeStruct((channels, points), F32),
         cost_estimate=pl.CostEstimate(flops=2_000_000_000, bytes_accessed=6_000_000, transcendentals=1_000_000),
@@ -324,17 +346,14 @@
     )
     start = (span + odd * beside.shape[0]).reshape(1)
     live = lax.broadcasted_iota(jnp.int32, (nodes, degree), 1) < mesh_degree[:, None]
-    place, live, named, index, outside, start, ids = lax.optimization_barrier(
-        (
-            place.reshape(-1, 1),
-            live.astype(F32).reshape(-1, 1),
-            named.reshape(-1, 1),
-            decoder_senders.reshape(-1, 1),
-            outside,
-            start,
-            ids,
-        )
-    )
+    columns = (
+        place.reshape(-1, 1),
+        live.astype(F32).reshape(-1, 1),
+        named.reshape(-1, 1),
+        decoder_senders.reshape(-1, 1),
+    )
+    columns, outside, start, ids = lax.optimization_barrier((kept(columns), outside, start, ids))
+    place, live, named, index = columns
     found = rows_of(table, ids)
     got = delivered(found)
     most, _ = lax.optimization_barrier((most, found))
@@ -346,6 +365,9 @@
         return matmul(late, delivered(rows_of(table, late_ids))).astype(BF16)
 
     extra = lax.cond(most > CAPACITY, fetch_rest, lambda: jnp.zeros((slots, width), BF16))
+    pe_first = weight(table, 0, 12)
+    next_table, _ = lax.optimization_barrier((table, pe_first))
+    got, de_first = lax.optimization_barrier((got, weight(next_table, 32, 12)))
     edge_out, mesh_out, copies = processor(
         place,
         live,
@@ -353,9 +375,10 @@
         extra,
         mesh_edges,
         mesh_latent,
-        weight(table, 0, 12),
+        pe_first,
         weight(table, 12, 4),
-        weight(table, 16, 8),
+        table.reshape(-1, stride, width),
+        nodes + 16,
         weight(table, 24, 4),
         2 * group,
     )
@@ -363,7 +386,6 @@
     late_table, _ = lax.optimization_barrier((table, mesh_out))
     near = two_patches(copies)
     far = swapped(matmul(one_hot(outside, near.shape[0]), near).astype(BF16), "wide", 1)
-    de_first = weight(late_table, 32, 12)
     first = decoder_first(named, index, near, decoder_edges, grid_latent, de_first)
     grid_pred = decoder_second(
         start,
@@ -374,7 +396,8 @@
         grid_latent,
         de_first,
         weight(late_table, 44, 4),
-        weight(late_table, 48, 8),
+        late_table.reshape(-1, stride, width),
+        nodes + 48,
         weight(late_table, 56, 4),
         weight(late_table, 28, 4)[:, :channels],
     ).T

time: 194 us -> 191 us (0.985)
  local copies, waits for them, and re-layouts: 41.3 us -> 36.4 us
  Pallas kernels: 21.3 us -> 23.5 us
    reshape x9 -> x7, local copies, waits for them, and re-layouts: 11.1 us -> 6.52 us  [weight(): return parts[:, nodes + first:nodes + first + count].reshape(-1, width)]
    all_to_all x1, waiting for transfers between devices: 0.01 us -> 3.09 us  [two_patches(): lax.all_to_all(copies, ('wide', 'narrow'), split_axis=0, concat_axis=0, a...]
    optimization_barrier x3 -> x0, local copies, waits for them, and re-layouts: 2.62 us -> none  [body(): lax.optimization_barrier((place.reshape(-1, 1), live.astype(F32).reshape(...]
    pallas_call x0 -> x1, Pallas kernels: none -> 2.23 us  [kept(): pl.pallas_call(keep_kernel, out_shape=[jax.ShapeDtypeStruct(c.shape, c.dt...]
    all_gather x1, waiting for transfers between devices: 42.6 us -> 40.5 us  [body(): table = lax.all_gather(pack, 'wide', axis=0, tiled=True)]
    unnamed x10 -> x12, local copies, waits for them, and re-layouts: 4.53 us -> 4.51 us
  transfers between devices with their start and end apart: 8 -> 8, of which waited for: 5 -> 6; matrix products, arithmetic and copies ran while one was open for 17% -> 15% of each run, Pallas kernels for 3% -> 4%
where the time goes in v4:
time: 191 us; the launch traced here: 190 us
  waiting for transfers between devices  62.2 us (33%)
  starting transfers between devices  47 us (25%)
  local copies, waits for them, and re-layouts  36.4 us (19%)
  Pallas kernels  23.5 us (12%)
  between operations  15.6 us (8%)
  other arithmetic  4.16 us (2%)
    all_gather x1, waiting for transfers between devices, body(): table = lax.all_gather(pack, 'wide', axis=0, tiled=True)  40.5 us
    all_to_all x4, starting transfers between devices, exchanged(): return lax.all_to_all(blocks, axis, split_axis=0, concat_axis=0, tiled=True)  34.8 us
    all_to_all x4, waiting for transfers between devices, exchanged(): return lax.all_to_all(blocks, axis, split_axis=0, concat_axis=0, tiled=True)  18.7 us
    gather x1, local copies, waits for them, and re-layouts, rows_of(): return table.at[ids].get(mode='promise_in_bounds')  11.3 us
    slice x4, local copies, waits for them, and re-layouts, weight(): return parts[:, nodes + first:nodes + first + count].reshape(-1, width)  8.06 us
    ppermute x2, starting transfers between devices, swapped(): return lax.ppermute(block, axis, pairs)  7.34 us
    pallas_call x1, Pallas kernels, processor(): pl.pallas_call(processor_kernel, grid=(steps,), in_specs=[tiles(place), t...  7.26 us
    pallas_call x1, Pallas kernels, decoder_second(): pl.pallas_call(decoder_second_kernel, grid=(steps,), in_specs=[pl.BlockSp...  7.09 us
  transfers between devices with their start and end apart: 8, of which 6 were waited for; matrix products, arithmetic and copies ran while one was open for 15% of the time, Pallas kernels for 4%

profile of v4, /device:TPU:2, one launch (start us, length us, event | category | flops | bytes accessed | tf_op | source)
XLA Modules:
  0.0 190.4 jit_solution(13745622347627017579)
XLA Ops:
  7.2 1.6 pack.1
  9.6 1.9 %collective-permute-start = (s32[32]{0:T(128)S(1)}, s32[32]{0:T(128)S(1)}, u32[]{:S(2)}, u32[]{:S(2)}) collective-permute-start(s32[32]{0:T(128)S(1)} %get-tuple-element.147), channel_id=1, source_target_pairs={{0,4},{4,0},{8,12},{12,8},{16,20},{20,16},{24,28},{28,24},{32,36},... | collective-permute-start | bytes 392 | tf_op jit(solution)/shard_map/ppermute | solution.py:222
  11.5 1.4 copy.81
  13.0 17.9 %all-to-all-start.2 = ((s32[128,1,32]{2,1,0:T(1,128)}), s32[128,1,32]{2,1,0:T(1,128)S(1)}, u32[]{:S(2)}, u32[]{:S(2)}) async-start(s32[128,1,32]{2,1,0:T(1,128)} %bitcast.2), calls=%async_computation.2 | async-start | bytes 131072 | tf_op jit(solution)/shard_map/all_to_all | solution.py:216
  32.8 0.9 reshape.454.refs_3_
  35.5 6.5 %all-to-all-done.2 = s32[128,1,32]{2,1,0:T(1,128)S(1)} async-done(((s32[128,1,32]{2,1,0:T(1,128)}), s32[128,1,32]{2,1,0:T(1,128)S(1)}, u32[]{:S(2)}, u32[]{:S(2)}) %all-to-all-start.2) | async-done | bytes 16416 | tf_op jit(solution)/shard_map/all_to_all | solution.py:216
  45.6 4.8 %all-to-all-start.3 = ((s32[4,1,384]{2,1,0:T(1,128)}), s32[4,1,384]{2,1,0:T(1,128)S(1)}, u32[]{:S(2)}, u32[]{:S(2)}) async-start(s32[4,1,384]{2,1,0:T(1,128)} %all_to_all.37), calls=%async_computation.3 | async-start | bytes 12288 | tf_op jit(solution)/shard_map/all_to_all | solution.py:216
  50.4 0.9 fusion.29.refs_0_
  51.3 2.2 %columns.1 = (s32[512,1]{1,0:T(8,128)}, f32[512,1]{1,0:T(8,128)}, s32[320,1]{1,0:T(8,128)}, s32[768,1]{1,0:T(8,128)}) custom-call(s32[512,1]{1,0:T(8,128)} %fusion.29.refs_0_, f32[512,1]{1,0:T(8,128)} %reshape.452.refs_1_, s32[320,1]{1,0:T(8,128)} %reshape.453.refs_2_, s32[768,1]{1,0:T(8,128)} %reshape.454.refs_3_), custom_call_target="tpu_custom_call" | custom-call | tf_op jit(solution)/shard_map/columns/pallas_call | solution.py:67
  55.0 1.3 broadcast_in_dim.63
  56.3 7.3 %all-to-all-start.5 = ((s32[128,1,8]{2,1,0:T(1,128)}), s32[128,1,8]{2,1,0:T(1,128)S(1)}, u32[]{:S(2)}, u32[]{:S(2)}) async-start(s32[128,1,8]{2,1,0:T(1,128)} %broadcast_in_dim.63), calls=%async_computation.5 | async-start | bytes 131072 | tf_op jit(solution)/shard_map/all_to_all | solution.py:216
  63.6 11.1 %all-to-all-done.5 = s32[128,1,8]{2,1,0:T(1,128)S(1)} async-done(((s32[128,1,8]{2,1,0:T(1,128)}), s32[128,1,8]{2,1,0:T(1,128)S(1)}, u32[]{:S(2)}, u32[]{:S(2)}) %all-to-all-start.5) | async-done | bytes 4128 | tf_op jit(solution)/shard_map/all_to_all | solution.py:216
  75.5 40.5 %all-gather.2.cloned.1.call-done = bf16[16384,512]{1,0:T(8,128)(2,1)} async-done(((bf16[128,512]{1,0:T(8,128)(2,1)}), bf16[16384,512]{1,0:T(8,128)(2,1)}) %all-gather.2.cloned.1.call-update) | async-done | bytes 16777232 | tf_op jit(solution)/shard_map/all_gather | solution.py:324
  115.9 11.3 %gather_fusion.1 = bf16[704,512]{1,0:T(8,128)(2,1)} fusion(bf16[16384,512]{1,0:T(8,128)(2,1)} %all-gather.2.cloned.1.call-done, s32[1024]{0:T(1024)S(1)} %pad_clamp_fusion.1), kind=kCustom, calls=%fused_computation.1 | custom fusion | bytes 1444608 | tf_op jit(solution)/shard_map/gather | solution.py:273
  128.2 4.8 %all-to-all-start.4 = ((bf16[4,176,512]{2,1,0:T(8,128)(2,1)}), bf16[4,176,512]{2,1,0:T(8,128)(2,1)S(1)}, u32[]{:S(2)}, u32[]{:S(2)}) async-start(bf16[4,176,512]{2,1,0:T(8,128)(2,1)} %bitcast.10), calls=%async_computation.4 | async-start | bytes 1441792 | tf_op jit(solution)/shard_map/all_to_all | solution.py:216
  133.0 1.8 slice.77
  134.7 1.4 reshape.424.w_first
  136.1 1.8 slice.78
  137.9 1.4 reshape.426.w_first.w_send
  139.2 2.0 %fusion.55 = (bf16[128,4,512]{2,1,0:T(4,128)(2,1)S(1)}, bf16[128,4,512]{2,1,0:T(4,128)(2,1)S(1)}) fusion(bf16[128,128,512]{2,1,0:T(8,128)(2,1)} %bitcast.31), kind=kLoop, calls=%fused_computation.122 | loop fusion | bytes 2097152 | tf_op jit(solution)/shard_map/slice | solution.py:328
  141.2 0.9 reshape.427.w_second
  142.1 0.9 reshape.428.n_second
  143.5 0.9 copy-done
  144.4 7.3 %processor.1 = (bf16[512,512]{1,0:T(8,128)(2,1)}, bf16[64,512]{1,0:T(8,128)(2,1)}, bf16[8,64,512]{2,1,0:T(8,128)(2,1)}) custom-call(s32[512,1]{1,0:T(8,128)} %get-tuple-element.112.place, f32[512,1]{1,0:T(8,128)} %get-tuple-element.113.live, bf16[704,512]{1,0:T(8,128)(2,1)} %bitcast.36, bf16[512,512]{1,0:T(8,128)(2,1)S(1)} %get-tuple-element.152.extra, ...), custom_call_target="tpu_custom_call" | custom-call | flops 2000000000 | bytes 8000000 | tf_op jit(solution)/shard_map/processor/pallas_call | solution.py:110
  151.6 4.9 %all-to-all-start.6 = ((bf16[8,64,512]{2,1,0:T(8,128)(2,1)}), bf16[8,64,512]{2,1,0:T(8,128)(2,1)S(1)}, u32[]{:S(2)}, u32[]{:S(2)}) async-start(bf16[8,64,512]{2,1,0:T(8,128)(2,1)} %get-tuple-element.123), calls=%async_computation.6 | async-start | bytes 1048576 | tf_op jit(solution)/shard_map/all_to_all | solution.py:290
  156.5 2.5 %fusion.54 = (bf16[128,4,512]{2,1,0:T(4,128)(2,1)S(1)}, bf16[128,4,512]{2,1,0:T(4,128)(2,1)S(1)}, bf16[128,4,512]{2,1,0:T(4,128)(2,1)S(1)}) fusion(bf16[128,128,512]{2,1,0:T(8,128)(2,1)} %bitcast.33), kind=kLoop, calls=%fused_computation.121 | loop fusion | bytes 3145728 | tf_op jit(solution)/shard_map/slice | solution.py:328
  159.9 0.9 reshape.431.w_second
  160.8 0.9 reshape.432.n_second
  161.8 3.1 %all-to-all-done.6 = bf16[8,64,512]{2,1,0:T(8,128)(2,1)S(1)} async-done(((bf16[8,64,512]{2,1,0:T(8,128)(2,1)}), bf16[8,64,512]{2,1,0:T(8,128)(2,1)S(1)}, u32[]{:S(2)}, u32[]{:S(2)}) %all-to-all-start.6) | async-done | bytes 524320 | tf_op jit(solution)/shard_map/all_to_all | solution.py:290
  165.1 5.4 %collective-permute-start.1 = (bf16[32,512]{1,0:T(8,128)(2,1)S(1)}, bf16[32,512]{1,0:T(8,128)(2,1)S(1)}, u32[]{:S(2)}, u32[]{:S(2)}) collective-permute-start(bf16[32,512]{1,0:T(8,128)(2,1)S(1)} %convolution_convert_fusion), channel_id=1, source_target_pairs={{4,8},{8,4},{12,16},{16,12},{20,24},{24,20},{28,32},{32,28},{36,40... | collective-permute-start | bytes 98312 | tf_op jit(solution)/shard_map/ppermute | solution.py:222
  170.5 5.4 %decoder_first.1.first = f32[768,512]{1,0:T(8,128)} custom-call(s32[320,1]{1,0:T(8,128)} %get-tuple-element.124.named, s32[768,1]{1,0:T(8,128)} %get-tuple-element.121.index, bf16[512,512]{1,0:T(8,128)(2,1)} %bitcast.38, bf16[768,512]{1,0:T(8,128)(2,1)} %edges.5, bf16[256,512]{1,0:T(8,128)(2,1)} %latent.5, bf16[1536,512]{1,0:T(8,128)(2,1)} %reshape.426.w_first.w_send), custom_call_target="tpu_custom_call" | custom-call | flops 2000000000 | bytes 6000000 | tf_op jit(solution)/shard_map/decoder_first/pallas_call | solution.py:151
  176.5 7.1 %decoder_second.1 = f32[227,256]{1,0:T(8,128)} custom-call(s32[1]{0:T(128)} %bitcast.8.start, s32[768,1]{1,0:T(8,128)} %get-tuple-element.121.index, bf16[32,512]{1,0:T(8,128)(2,1)} %copy-done.2, f32[768,512]{1,0:T(8,128)} %decoder_first.1.first, bf16[768,512]{1,0:T(8,128)(2,1)} %edges.5, bf16[256,512]{1,0:T(8,128)(2,1)} %latent.5, ...), custom_call_target="tpu_custom_call" | custom-call | flops 2000000000 | bytes 6000000 | tf_op jit(solution)/shard_map/decoder_second/pallas_call | solution.py:195
  (61 shorter events, 12.1 us)
Async XLA Ops:
  7.2 26.5 %copy-start.3 = (s32[64]{0:T(128)S(1)}, s32[64]{0:T(128)}, u32[]{:S(2)}) copy-start(s32[64]{0:T(128)} %param.25) | copy-start | bytes 772
  7.2 108.7 %all-gather.2.cloned.1.call-start = ((), (), s32[]{:S(2)}) async-start(), calls=%async_computation.7 | async-start | bytes 16908288 | tf_op jit(solution)/shard_map/all_gather | solution.py:324
  9.6 25.0 %collective-permute-start = (s32[32]{0:T(128)S(1)}, s32[32]{0:T(128)S(1)}, u32[]{:S(2)}, u32[]{:S(2)}) collective-permute-start(s32[32]{0:T(128)S(1)} %get-tuple-element.147), channel_id=1, source_target_pairs={{0,4},{4,0},{8,12},{12,8},{16,20},{20,16},{24,28},{28,24},{32,36},... | collective-permute-start | bytes 392 | tf_op jit(solution)/shard_map/ppermute | solution.py:222
  13.0 29.0 %all-to-all-start.2 = ((s32[128,1,32]{2,1,0:T(1,128)}), s32[128,1,32]{2,1,0:T(1,128)S(1)}, u32[]{:S(2)}, u32[]{:S(2)}) async-start(s32[128,1,32]{2,1,0:T(1,128)} %bitcast.2), calls=%async_computation.2 | async-start | bytes 131072 | tf_op jit(solution)/shard_map/all_to_all | solution.py:216
  45.6 8.7 %all-to-all-start.3 = ((s32[4,1,384]{2,1,0:T(1,128)}), s32[4,1,384]{2,1,0:T(1,128)S(1)}, u32[]{:S(2)}, u32[]{:S(2)}) async-start(s32[4,1,384]{2,1,0:T(1,128)} %all_to_all.37), calls=%async_computation.3 | async-start | bytes 12288 | tf_op jit(solution)/shard_map/all_to_all | solution.py:216
  56.3 18.4 %all-to-all-start.5 = ((s32[128,1,8]{2,1,0:T(1,128)}), s32[128,1,8]{2,1,0:T(1,128)S(1)}, u32[]{:S(2)}, u32[]{:S(2)}) async-start(s32[128,1,8]{2,1,0:T(1,128)} %broadcast_in_dim.63), calls=%async_computation.5 | async-start | bytes 131072 | tf_op jit(solution)/shard_map/all_to_all | solution.py:216
  128.2 15.3 %all-to-all-start.4 = ((bf16[4,176,512]{2,1,0:T(8,128)(2,1)}), bf16[4,176,512]{2,1,0:T(8,128)(2,1)S(1)}, u32[]{:S(2)}, u32[]{:S(2)}) async-start(bf16[4,176,512]{2,1,0:T(8,128)(2,1)} %bitcast.10), calls=%async_computation.4 | async-start | bytes 1441792 | tf_op jit(solution)/shard_map/all_to_all | solution.py:216
  143.5 0.9 copy-start
  151.6 13.2 %all-to-all-start.6 = ((bf16[8,64,512]{2,1,0:T(8,128)(2,1)}), bf16[8,64,512]{2,1,0:T(8,128)(2,1)S(1)}, u32[]{:S(2)}, u32[]{:S(2)}) async-start(bf16[8,64,512]{2,1,0:T(8,128)(2,1)} %get-tuple-element.123), calls=%async_computation.6 | async-start | bytes 1048576 | tf_op jit(solution)/shard_map/all_to_all | solution.py:290
  164.8 5.7 %copy-start.1 = (bf16[8,64,512]{2,1,0:T(8,128)(2,1)}, bf16[8,64,512]{2,1,0:T(8,128)(2,1)S(1)}, u32[]{:S(2)}) copy-start(bf16[8,64,512]{2,1,0:T(8,128)(2,1)S(1)} %all-to-all-done.6) | copy-start | bytes 1572868
  165.1 10.8 %collective-permute-start.1 = (bf16[32,512]{1,0:T(8,128)(2,1)S(1)}, bf16[32,512]{1,0:T(8,128)(2,1)S(1)}, u32[]{:S(2)}, u32[]{:S(2)}) collective-permute-start(bf16[32,512]{1,0:T(8,128)(2,1)S(1)} %convolution_convert_fusion), channel_id=1, source_target_pairs={{4,8},{8,4},{12,16},{16,12},{20,24},{24,20},{28,32},{32,28},{36,40... | collective-permute-start | bytes 98312 | tf_op jit(solution)/shard_map/ppermute | solution.py:222
  175.9 0.6 copy-start.2
Sparse Core Ops, SparseCore 0:
  11.1 104.7 all-gather.1
